TPU v7x, 32 devices: a whole 2x2x4 slice. The times are simulated.
32 devices in a mesh: dev: 32 (over z, y, x, core).
Axes of the slice: x: 2, y: 2, z: 4, core: 2. Of those that a mesh axis runs over, the one named last changes fastest.
Arguments:
- upstream: bfloat16 [16384, 1024], P('dev'), may hold values from -6 to 6
- bag: int32 [16384, 8], P('dev'), may hold values from 0 to 191
- next_bag: int32 [16384, 8], P('dev'), may hold values from 0 to 127
- hot_slots: int32 [4096], P('dev'), may hold values from 0 to 2047, as said below
- evict_dest: int32 [32, 32, 2], P('dev'), may hold values from -1 to 1023, as said below
- hot_cache: float32 [4096, 128], P('dev'), may hold values from -6 to 6
- evict_cache: float32 [2048, 128], P('dev'), may hold values from -6 to 6
- hot_table: float32 [2048, 128], P('dev'), may hold values from -6 to 6
- hot_accum: float32 [2048, 128], P('dev'), may hold values from 1 to 100
- owner_table: float32 [32768, 128], P('dev'), may hold values from -6 to 6
- owner_accum: float32 [32768, 128], P('dev'), may hold values from 1 to 30
- cross_w: float32 [2, 1024, 1024], P(None, None, 'dev'), may hold values from -0.1875 to 0.1875
- cross_b: float32 [2, 1024], P(None, 'dev'), may hold values from -3 to 3
- cross_accum: float32 [2, 1024, 1024], P(None, None, 'dev'), may hold values from 10000 to 1000000
Outputs:
- next_first: bfloat16 [16384, 1024], P('dev')
- hot_new: float32 [2048, 128], P('dev')
- hot_accum_new: float32 [2048, 128], P('dev')
- owner_new: float32 [32768, 128], P('dev')
- owner_accum_new: float32 [32768, 128], P('dev')
- cross_w_new: float32 [2, 1024, 1024], P(None, None, 'dev')
- cross_b_new: float32 [2, 1024], P(None, 'dev')
Inputs may be any that keep to these rules, and one draw needn't show every extreme that they name: `hot_slots`: entry d * 128 + 4 * o + k names a row of owner o's block, o * 64 to o * 64 + 63; the 4 rows of one device in one owner's block are distinct. evict_dest[o, s, k] is the row of owner o's block (0 to 1023) that receives the gradient of source s's evicted slot 2 * o + k, or -1 for an empty slot; in each (o, s) bucket the live entries come first, and some bucket is full in every draw.
All inputs are finite; a program needn't handle non-finite values.
Results may differ from a plain program's by a relative error of at most 0.0033.
The roundings to bfloat16 on the way count: a program that leaves them out, or rounds other values in their place, can miss the bound.
Values may be sent and summed in bfloat16 or wider, within the bound.
No kernel may reach another device: no remote copies, remote signals or barrier semaphores. Data moves between devices by JAX's collectives and lax.ppermute only.
A program may use at most 128 MiB of HBM per device.

v0:
```python
import math

import jax
import jax.numpy as jnp
import numpy as np
from jax import lax
from jax.experimental import pallas as pl
from jax.experimental.pallas import tpu as pltpu
from jax.sharding import PartitionSpec as P


row_rate = 0.05
weight_rate = 0.005
bias_rate = 0.0002
epsilon = 1e-10
f32 = jnp.float32
bf16 = jnp.bfloat16


def adagrad(params, accumulator, gradient, step_rate):
    updated = accumulator + gradient * gradient
    return (params - step_rate * gradient / (jnp.sqrt(updated) + epsilon), updated)


def bit_groups(devices):
    bits = devices.bit_length() - 1
    assert devices == 1 << bits
    return [(0, 1)] + [(low, min(2, bits - low)) for low in range(1, bits, 2)]


def group_masks(group):
    low, width = group
    return [value << low for value in range(1 << width)]


def relative_masks(devices):
    masks = [0]
    for group in reversed(bit_groups(devices)):
        masks = [own | inner for own in group_masks(group) for inner in masks]
    return np.array(masks, np.int32)


def swap(values, mask, devices):
    return lax.ppermute(values, "dev", [(i, i ^ mask) for i in range(devices)])


def after(values, *others):
    return lax.optimization_barrier((values, others))[0]


def gather_outer(block, devices):
    stack = block[None]
    for group in reversed(bit_groups(devices)[2:]):
        parts = [stack] + [swap(stack, mask, devices) for mask in group_masks(group)[1:]]
        stack = jnp.concatenate(parts, axis=0)
    return stack


def gather_near(stack, devices):
    masks = group_masks(bit_groups(devices)[1])[1:]
    near = [stack] + [swap(stack, mask, devices) for mask in masks]
    return near + [swap(part, 1, devices) for part in near]


def sum_stage(keep, parts, group, devices):
    total = keep.astype(f32)
    arrived = [swap(part, mask, devices) for part, mask in zip(parts, group_masks(group)[1:])]
    for part in arrived:
        total = total + part.astype(f32)
    return total, arrived


def parts_of(stack, group):
    parts = stack.reshape(len(group_masks(group)), -1, *stack.shape[1:])
    return parts[0], [parts[k].astype(bf16) for k in range(1, parts.shape[0])]


def to_absolute(parts, my_index, devices):
    stack = jnp.concatenate(parts, axis=0)
    place = np.argsort(relative_masks(devices)).astype(np.int32)
    order = jnp.asarray(place)[jnp.arange(devices, dtype=jnp.int32) ^ my_index]
    return jnp.take(stack, order, axis=0, mode="clip").reshape(-1, stack.shape[-1])


def to_relative(blocks, my_index, devices):
    order = jnp.asarray(relative_masks(devices)) ^ my_index
    return jnp.take(blocks, order, axis=0, mode="clip")


def dot(a, b, ca, cb):
    return lax.dot_general(a, b, (((ca,), (cb,)), ((), ())), preferred_element_type=f32)


def exchange(values):
    return lax.all_to_all(values, "dev", split_axis=0, concat_axis=0, tiled=True)


def one_hot(index_row, rows):
    samples = index_row.shape[1]
    return (index_row == lax.broadcasted_iota(jnp.int32, (rows, samples), 0)).astype(bf16)


def high_low(table):
    high = table.astype(bf16)
    return jnp.concatenate([high, (table - high.astype(f32)).astype(bf16)], axis=1)


def call(body, outs, inputs, scratch=(), loose=()):
    vmem = pl.BlockSpec(memory_space=pltpu.VMEM)
    count = len(inputs)

    def kernel(*refs):
        body(*refs[:count], *refs[count + len(loose) :])

    return pl.pallas_call(
        kernel,
        out_shape=[jax.ShapeDtypeStruct(*out) for out in outs],
        in_specs=[pl.BlockSpec(memory_space=pltpu.SMEM)]
        + [vmem] * (count - 1)
        + [pl.BlockSpec(memory_space=pl.ANY)] * len(loose),
        out_specs=[vmem] * len(outs),
        scratch_shapes=[pltpu.VMEM(*shape) for shape in scratch],
    )(*inputs, *loose)


def put_parts(parts, target, my_index, masks):
    place = 0
    for part in parts:
        for k in range(part.shape[0]):
            target[masks[place] ^ my_index] = part[k]
            place += 1


def give_halves(blocks, keep, send, my_index, masks):
    half = len(masks) // 2
    for place in range(half):
        keep[place] = blocks[masks[place] ^ my_index]
        send[place] = blocks[masks[half + place] ^ my_index].astype(bf16)


def chunks(rows):
    step = math.gcd(rows, 256)
    return [slice(at, at + step) for at in range(0, rows, step)]


def pick(me, index, table, loose=()):
    fields, samples = index.shape
    rows, width = table.shape

    def body(me_ref, index_ref, table_ref, out):
        both = high_low(table_ref[...])
        for k in range(fields):
            picked = dot(one_hot(index_ref[k : k + 1, :], rows), both, 0, 0)
            out[:, k * width : (k + 1) * width] = picked[:, :width] + picked[:, width:]

    return call(body, [((samples, fields * width), f32)], [me, index, table], loose=loose)[0]


def step_two(me, masks, parts, upstream, feat):
    n, r, depth = len(masks), parts[0].shape[1], feat.shape[1]
    samples = feat.shape[0]

    def body(me_ref, up, feat_ref, *refs):
        refs = list(refs)
        part_refs, refs = refs[: len(parts)], refs[len(parts) :]
        bias, keep, send, w1, one_bf, feat_bf, grads = refs
        mine = me_ref[0]
        put_parts(part_refs, w1, mine, masks)
        weights = w1[...].reshape(n * r, depth)
        total = jnp.zeros((1, depth), f32)
        for at in chunks(samples):
            g = up[at].astype(f32)
            f = feat_ref[at]
            feat_bf[at] = f.astype(bf16)
            grad_layer = g + dot((g * f).astype(bf16), weights, 1, 0)
            grad_one = grad_layer * f
            total = total + jnp.sum(grad_one, axis=0, keepdims=True)
            one_bf[at] = grad_one.astype(bf16)
        bias[...] = total
        grads[...] = dot(one_bf[...], feat_bf[...], 0, 0).reshape(n, r, depth)
        give_halves(grads, keep, send, mine, masks)

    return call(
        body,
        [
            ((1, depth), f32),
            ((n // 2, r, depth), f32),
            ((n // 2, r, depth), bf16),
        ],
        [me, upstream, feat, *parts],
        [
            ((n, r, depth), bf16),
            ((samples, depth), bf16),
            ((samples, depth), bf16),
            ((n, r, depth), f32),
        ],
    )


def iota(shape, dim):
    return lax.broadcasted_iota(jnp.int32, shape, dim)


def log2(count):
    assert count & (count - 1) == 0
    return count.bit_length() - 1


class Packing:
    def __init__(self, devices, shared, evicted, columns):
        self.devices, self.shared, self.evicted = devices, shared, evicted
        self.columns = columns
        self.bias_row = shared + evicted
        self.each = 8 << max(0, (self.bias_row // 8).bit_length())
        self.total = devices * self.each

    def pack(self, slot_sum, biases):
        width = slot_sum.shape[1]
        shape = (self.total, slot_sum.shape[0])
        device, row = iota(shape, 0) >> log2(self.each), iota(shape, 0) & (self.each - 1)
        evict = self.devices * self.shared + device * self.evicted + row - self.shared
        slot = jnp.where(row < self.shared, device * self.shared + row, evict)
        slot = jnp.where(row < self.bias_row, slot, -1)
        chosen = (slot == iota(shape, 1)).astype(bf16)
        packed = halves_sum(dot(chosen, high_low(slot_sum), 1, 0), width)
        spread = jnp.zeros((self.devices, width), f32)
        for layer, bias in enumerate(biases):
            depth = bias.shape[1]
            shape = (self.devices, depth)
            own = jnp.where(iota(shape, 1) >> log2(self.columns) == iota(shape, 0), bias, 0.0)
            shape = (depth, width)
            lane = (iota(shape, 0) & (self.columns - 1)) + layer * self.columns
            to = (lane == iota(shape, 1)).astype(bf16)
            high = own.astype(bf16)
            low = (own - high.astype(f32)).astype(bf16)
            spread = spread + dot(high, to, 1, 0) + dot(low, to, 1, 0)
        shape = (self.total, self.devices)
        here = iota(shape, 0) == (iota(shape, 1) << log2(self.each)) + self.bias_row
        return packed + halves_sum(dot(here.astype(bf16), high_low(spread), 1, 0), width)

    def rows(self, values, at):
        after_them = self.each - at - values.shape[1]
        spaced = jnp.pad(values, ((0, 0), (at, after_them)), constant_values=-1)
        return spaced.reshape(1, -1)


def step_four(me, masks, parts, parts1, upstream, feat, biases, index, slots, bias1, packing, loose):
    n, r, depth = len(masks), parts[0].shape[1], feat.shape[1]
    samples, fields = feat.shape[0], index.shape[0]
    width = depth // fields

    def body(me_ref, up, feat_ref, biases_ref, index_ref, bias1_ref, *refs):
        refs = list(refs)
        count = len(parts)
        packed, keep, send, w0, w1, layer_bf, two_bf, feat_grad, grads = refs[2 * count :]
        mine = me_ref[0]
        put_parts(refs[:count], w0, mine, masks)
        put_parts(refs[count : 2 * count], w1, mine, masks)
        first = w0[...].reshape(n * r, depth)
        second = w1[...].reshape(n * r, depth)
        total = jnp.zeros((1, depth), f32)
        for at in chunks(samples):
            g = up[at].astype(f32)
            f = feat_ref[at]
            two = g * f
            total = total + jnp.sum(two, axis=0, keepdims=True)
            two_bf[at] = two.astype(bf16)
            proj_one = dot(f.astype(bf16), first, 1, 1) + biases_ref[0:1]
            layer_bf[at] = (f * proj_one + f).astype(bf16)
            proj_two = dot(layer_bf[at], second, 1, 1) + biases_ref[1:2]
            layer = g + dot(two_bf[at], second, 1, 0)
            grad_feat = g * proj_two + layer * (proj_one + 1.0)
            grad_feat = grad_feat + dot((layer * f).astype(bf16), first, 1, 0)
            feat_grad[at] = grad_feat.astype(bf16)
        slot_sum = jnp.zeros((slots, width), f32)
        for k in range(fields):
            block = feat_grad[:, k * width : (k + 1) * width]
            slot_sum = slot_sum + dot(one_hot(index_ref[k : k + 1, :], slots), block, 1, 0)
        packed[...] = packing.pack(slot_sum, (bias1_ref[...], total))
        grads[...] = dot(two_bf[...], layer_bf[...], 0, 0).reshape(n, r, depth)
        give_halves(grads, keep, send, mine, masks)

    return call(
        body,
        [
            ((packing.total, width), f32),
            ((n // 2, r, depth), f32),
            ((n // 2, r, depth), bf16),
        ],
        [me, upstream, feat, biases, index, bias1, *parts, *parts1],
        [
            ((n, r, depth), bf16),
            ((n, r, depth), bf16),
            ((samples, depth), bf16),
            ((samples, depth), bf16),
            ((samples, depth), bf16),
            ((n, r, depth), f32),
        ],
        loose,
    )


def step_six(me, masks, parts, feat, bias):
    n, r, depth = len(masks), parts[0].shape[1], feat.shape[1]
    samples = feat.shape[0]

    def body(me_ref, feat_ref, bias_ref, *refs):
        part_refs, (out, wn) = refs[: len(parts)], refs[len(parts) :]
        put_parts(part_refs, wn, me_ref[0], masks)
        weights = wn[...].reshape(n * r, depth)
        for at in chunks(samples):
            f = feat_ref[at]
            proj = dot(f.astype(bf16), weights, 1, 1) + bias_ref[...]
            out[at] = (f * proj + f).astype(bf16)

    return call(
        body, [((samples, depth), bf16)], [me, feat, bias, *parts], [((n, r, depth), bf16)]
    )[0]


def halves_sum(both, width):
    return both[:, :width] + both[:, width:]


def hot_update(me, rows, arrived, table, accum, bias, packing):
    width = table.shape[1]

    def body(me_ref, rows_ref, arrived_ref, table_ref, accum_ref, bias_ref, *outs):
        new, accum_new, returned, bias_new = outs
        values = arrived_ref[...]
        place = iota(values.shape, 0) & (packing.each - 1)
        bias_sum = jnp.where(place == packing.bias_row, values, 0.0)
        bias_sum = jnp.sum(bias_sum, axis=0, keepdims=True)
        stepped = bias_ref[...] - bias_rate * bias_sum
        bias_new[...] = stepped
        chosen = one_hot(rows_ref[...], table.shape[0])
        gradient = halves_sum(dot(chosen, high_low(values), 1, 0), width)
        updated, accum_new[...] = adagrad(table_ref[...], accum_ref[...], gradient, row_rate)
        new[...] = updated
        back = halves_sum(dot(chosen, high_low(updated), 0, 0), width)
        returned[...] = jnp.where(
            place == packing.bias_row, stepped.astype(bf16).astype(f32), back
        )

    return call(
        body,
        [(table.shape, f32), (table.shape, f32), (arrived.shape, f32), ((1, width), f32)],
        [me, rows, arrived, table, accum, bias],
    )


def pick_next(me, index, table, packing, depth):
    fields, samples = index.shape
    rows, width = table.shape

    def body(me_ref, index_ref, table_ref, out, bias):
        values = table_ref[...]
        both = high_low(values)
        for k in range(fields):
            picked = dot(one_hot(index_ref[k : k + 1, :], rows), both, 0, 0)
            out[:, k * width : (k + 1) * width] = halves_sum(picked, width)
        shape = (width, depth)
        lanes = (iota(shape, 1) & (packing.columns - 1)) == iota(shape, 0)
        spread = dot(values.astype(bf16), lanes.astype(bf16), 1, 0)
        shape = (rows, depth)
        device = iota(shape, 1) >> log2(packing.columns)
        here = iota(shape, 0) == (device << log2(packing.each)) + packing.bias_row
        bias[...] = jnp.sum(jnp.where(here, spread, 0.0), axis=0, keepdims=True)

    return call(body, [((samples, depth), f32), ((1, depth), f32)], [me, index, table])


def owner_update(me, rows, moved, table, accum):
    width = table.shape[1]

    def body(me_ref, rows_ref, moved_ref, table_ref, accum_ref, new, accum_new):
        chosen = one_hot(rows_ref[...], table.shape[0])
        gradient = halves_sum(dot(chosen, high_low(moved_ref[...]), 1, 0), width)
        new[...], accum_new[...] = adagrad(table_ref[...], accum_ref[...], gradient, row_rate)

    return call(body, [(table.shape, f32), (table.shape, f32)], [me, rows, moved, table, accum])


def plain_halves(grads, me, masks):
    n = len(masks)
    placed = to_relative(grads.reshape(n, -1, grads.shape[1]), me[0], n)
    return placed[: n // 2], placed[n // 2 :].astype(bf16)


def plain_two(me, masks, parts, upstream, feat):
    w1 = to_absolute(parts, me[0], len(masks))
    g = upstream.astype(f32)
    layer = g + dot((g * feat).astype(bf16), w1, 1, 0)
    grad_one = layer * feat
    one_bf = grad_one.astype(bf16)
    keep, send = plain_halves(dot(one_bf, feat.astype(bf16), 0, 0), me, masks)
    return jnp.sum(grad_one, axis=0, keepdims=True), keep, send


def plain_four(me, masks, parts, parts1, upstream, feat, biases, index, slots, bias1, packing, loose):
    w0 = to_absolute(parts, me[0], len(masks))
    w1 = to_absolute(parts1, me[0], len(masks))
    g = upstream.astype(f32)
    two = g * feat
    proj_one = dot(feat.astype(bf16), w0, 1, 1) + biases[0:1]
    layer_bf = (feat * proj_one + feat).astype(bf16)
    proj_two = dot(layer_bf, w1, 1, 1) + biases[1:2]
    layer = g + dot(two.astype(bf16), w1, 1, 0)
    one_bf = (layer * feat).astype(bf16)
    grad_feat = g * proj_two + layer * (proj_one + 1.0) + dot(one_bf, w0, 1, 0)
    grad_feat = grad_feat.astype(bf16)
    width = feat.shape[1] // index.shape[0]
    slot = sum(
        dot(one_hot(row[None], slots), grad_feat[:, k * width : (k + 1) * width], 1, 0)
        for k, row in enumerate(index)
    )
    keep, send = plain_halves(dot(two.astype(bf16), layer_bf, 0, 0), me, masks)
    packed = packing.pack(slot, (bias1, jnp.sum(two, axis=0, keepdims=True)))
    return packed, keep, send


def plain_six(me, masks, parts, feat, bias):
    wn = to_absolute(parts, me[0], len(masks))
    proj = dot(feat.astype(bf16), wn, 1, 1) + bias
    return (feat * proj + feat).astype(bf16)


def local(
    upstream,
    bag,
    next_bag,
    hot_slots,
    evict_dest,
    hot_cache,
    evict_cache,
    hot_table,
    hot_accum,
    owner_table,
    owner_accum,
    cross_w,
    cross_b,
    cross_accum,
):
    n = lax.axis_size("dev")
    me = lax.axis_index("dev")
    width = hot_cache.shape[1]
    hot_count = hot_cache.shape[0]
    slots = hot_count + evict_cache.shape[0]
    columns = cross_b.shape[1]

    place = me.astype(jnp.int32).reshape(1)
    masks = [int(mask) for mask in relative_masks(n)]
    groups = bit_groups(n)
    if columns % 16 == 0 and bag.shape[0] % 128 == 0:
        two, four, six = step_two, step_four, step_six
    else:
        two, four, six = plain_two, plain_four, plain_six

    w_own = cross_w.transpose(0, 2, 1)
    w1_outer = gather_outer(w_own[1].astype(bf16), n)
    w1_parts = gather_near(w1_outer, n)
    w0_outer = gather_outer(after(w_own[0].astype(bf16), w1_outer), n)
    w0_parts = gather_near(after(w0_outer, *w1_parts[: len(w1_parts) // 2]), n)

    ids = hot_slots.reshape(n, -1)
    per = ids.shape[1]
    biases_own = cross_b.astype(bf16).astype(f32).reshape(1, -1)
    first = exchange(
        after(
            jnp.concatenate(
                [ids.astype(f32), jnp.broadcast_to(biases_own, (n, 2 * columns))], axis=1
            ),
            w1_outer,
        ),
    )
    arrived_ids = first[:, :per].astype(jnp.int32)
    biases = first[:, per:].reshape(n, 2, columns).transpose(1, 0, 2).reshape(2, -1)

    slot_values = jnp.concatenate([hot_cache, evict_cache], axis=0)
    feat = pick(place, bag.T, slot_values)

    def near_sum(keep, send):
        total, _ = sum_stage(keep, [send], groups[0], n)
        return parts_of(total, groups[1])

    def own_sum(total):
        for group in groups[2:]:
            keep, parts = parts_of(total, group)
            total, _ = sum_stage(keep, parts, group, n)
        return total[0]

    feat = after(feat, w0_outer)
    bias_one, keep0, send0 = two(place, masks, w1_parts, upstream, feat)
    keep0, parts0 = near_sum(keep0, send0)
    packing = Packing(n, per, evict_dest.shape[2], columns)
    packed, keep1, send1 = four(
        place,
        masks,
        w0_parts,
        w1_parts,
        upstream,
        feat,
        biases,
        bag.T,
        slots,
        bias_one,
        packing,
        parts0,
    )
    total0, arrived0 = sum_stage(keep0, parts0, groups[1], n)
    grad0 = own_sum(total0)
    w_new0, _ = adagrad(w_own[0], cross_accum.transpose(0, 2, 1)[0], grad0, weight_rate)
    w_next = w_new0.astype(bf16)
    wn_outer = gather_outer(w_next, n)
    wn_parts = gather_near(wn_outer, n)

    keep1, parts1 = near_sum(keep1, send1)
    total1, _ = sum_stage(keep1, after(parts1, *arrived0), groups[1], n)
    grad1 = own_sum(after(total1, wn_outer))
    w_new1, _ = adagrad(w_own[1], cross_accum.transpose(0, 2, 1)[1], grad1, weight_rate)

    arrived = exchange(packed.reshape(n, -1, width)).reshape(-1, width)
    local_rows = packing.rows(arrived_ids - me * hot_table.shape[0], 0)
    bias_lanes = jnp.pad(cross_b.reshape(1, -1), ((0, 0), (0, width - 2 * columns)))
    hot_new, hot_accum_new, returned, bias_new = hot_update(
        place, local_rows, arrived, hot_table, hot_accum, bias_lanes, packing
    )
    cross_b_new = bias_new[:, : 2 * columns].reshape(2, columns)
    back = exchange(returned.reshape(n, -1, width)).reshape(-1, width)
    owner_new, owner_accum_new = owner_update(
        place, packing.rows(evict_dest[0], per), arrived, owner_table, owner_accum
    )

    next_rows = (next_bag // per) * packing.each + next_bag % per
    next_feat, next_bias = pick_next(place, next_rows.T, back, packing, feat.shape[1])
    next_first = six(place, masks, wn_parts, next_feat, next_bias)
    cross_w_new = jnp.stack([w_new0, w_new1]).transpose(0, 2, 1)
    return (
        next_first,
        hot_new,
        hot_accum_new,
        owner_new,
        owner_accum_new,
        cross_w_new,
        cross_b_new,
    )


def solution(mesh):
    return jax.shard_map(
        local,
        mesh=mesh,
        in_specs=(
            P("dev", None),
            P("dev", None),
            P("dev", None),
            P("dev"),
            P("dev", None, None),
            P("dev", None),
            P("dev", None),
            P("dev", None),
            P("dev", None),
            P("dev", None),
            P("dev", None),
            P(None, None, "dev"),
            P(None, "dev"),
            P(None, None, "dev"),
        ),
        out_specs=(
            P("dev", None),
            P("dev", None),
            P("dev", None),
            P("dev", None),
            P("dev", None),
            P(None, None, "dev"),
            P(None, "dev"),
        ),
        check_vma=False,
    )
```

profile of v0, /device:TPU:0, one launch (start us, length us, event | category | flops | bytes accessed | tf_op | source)
XLA Modules:
  0.0 155.1 jit_solution(790100968758813881)
XLA Ops:
  0.6 1.0 fusion.14
  1.6 3.1 %collective-permute-start = (bf16[1,32,1024]{2,1,0:T(8,128)(2,1)S(1)}, bf16[1,32,1024]{2,1,0:T(8,128)(2,1)S(1)}, u32[]{:S(2)}, u32[]{:S(2)}) collective-permute-start(bf16[1,32,1024]{2,1,0:T(8,128)(2,1)S(1)} %get-tuple-element.72), channel_id=1, source_target_pairs={{0,8},{1,9},{2,10},{3,11},{4,12},{5,13},{6,14},{7,15},{8,0},{9,1},... | collective-permute-start | bytes 196616 | tf_op jit(solution)/shard_map/ppermute | solution.py:44
  4.7 2.6 %collective-permute-start.1 = (bf16[1,32,1024]{2,1,0:T(8,128)(2,1)S(1)}, bf16[1,32,1024]{2,1,0:T(8,128)(2,1)S(1)}, u32[]{:S(2)}, u32[]{:S(2)}) collective-permute-start(bf16[1,32,1024]{2,1,0:T(8,128)(2,1)S(1)} %get-tuple-element.72), channel_id=1, source_target_pairs={{0,16},{1,17},{2,18},{3,19},{4,20},{5,21},{6,22},{7,23},{8,24},{9,... | collective-permute-start | bytes 196616 | tf_op jit(solution)/shard_map/ppermute | solution.py:44
  7.3 4.7 %collective-permute-done.1 = bf16[1,32,1024]{2,1,0:T(8,128)(2,1)S(1)} collective-permute-done((bf16[1,32,1024]{2,1,0:T(8,128)(2,1)S(1)}, bf16[1,32,1024]{2,1,0:T(8,128)(2,1)S(1)}, u32[]{:S(2)}, u32[]{:S(2)}) %collective-permute-start.1) | collective-permute-done | bytes 65568 | tf_op jit(solution)/shard_map/ppermute | solution.py:44
  12.0 1.4 collective-permute-done.2
  13.5 1.6 %collective-permute-start.6 = (bf16[4,32,1024]{2,1,0:T(8,128)(2,1)S(1)}, bf16[4,32,1024]{2,1,0:T(8,128)(2,1)S(1)}, u32[]{:S(2)}, u32[]{:S(2)}) collective-permute-start(bf16[4,32,1024]{2,1,0:T(8,128)(2,1)S(1)} %pad_maximum_fusion.refs_3_.refs_14_), channel_id=1, source_target_pairs={{0,2},{1,3},{2,0},{3,1},{4,6},{5,7},{6,4},{7,5},{8,10},{9,11},{10,... | collective-permute-start | bytes 786440 | tf_op jit(solution)/shard_map/ppermute | solution.py:44
  15.0 1.5 collective-permute-start.7
  17.0 2.3 %collective-permute-start.4 = (bf16[1,32,1024]{2,1,0:T(8,128)(2,1)S(1)}, bf16[1,32,1024]{2,1,0:T(8,128)(2,1)S(1)}, u32[]{:S(2)}, u32[]{:S(2)}) collective-permute-start(bf16[1,32,1024]{2,1,0:T(8,128)(2,1)S(1)} %bitcast.30), channel_id=1, source_target_pairs={{0,16},{1,17},{2,18},{3,19},{4,20},{5,21},{6,22},{7,23},{8,24},{9,... | collective-permute-start | bytes 196616 | tf_op jit(solution)/shard_map/ppermute | solution.py:44
  19.4 1.9 %collective-permute-done.3 = bf16[1,32,1024]{2,1,0:T(8,128)(2,1)S(1)} collective-permute-done((bf16[1,32,1024]{2,1,0:T(8,128)(2,1)S(1)}, bf16[1,32,1024]{2,1,0:T(8,128)(2,1)S(1)}, u32[]{:S(2)}, u32[]{:S(2)}) %collective-permute-start.3) | collective-permute-done | bytes 65568 | tf_op jit(solution)/shard_map/ppermute | solution.py:44
  21.3 1.4 collective-permute-done.6.refs_4_.refs_15_
  22.7 4.1 %collective-permute-done.7.refs_5_.refs_16_ = bf16[4,32,1024]{2,1,0:T(8,128)(2,1)S(1)} collective-permute-done((bf16[4,32,1024]{2,1,0:T(8,128)(2,1)S(1)}, bf16[4,32,1024]{2,1,0:T(8,128)(2,1)S(1)}, u32[]{:S(2)}, u32[]{:S(2)}) %collective-permute-start.7) | collective-permute-done | bytes 262176 | tf_op jit(solution)/shard_map/ppermute | solution.py:44
  27.3 1.0 collective-permute-start.5
  28.3 1.5 pad_maximum_fusion.3.refs_2_
  29.8 3.0 %shard_map.189.refs_2_ = f32[512,1024]{1,0:T(8,128)} custom-call(s32[1]{0:T(128)} %bitcast.refs_0_, s32[8,512]{1,0:T(8,128)} %bitcast.37, f32[192,128]{1,0:T(8,128)} %pad_maximum_fusion.3.refs_2_), custom_call_target="tpu_custom_call" | custom-call | tf_op jit(solution)/shard_map/pallas_call | solution.py:115
  34.4 0.7 copy-done.13
  35.1 6.8 %shard_map.190 = (f32[1,1024]{1,0:T(1,128)}, f32[16,32,1024]{2,1,0:T(8,128)}, bf16[16,32,1024]{2,1,0:T(8,128)(2,1)}) custom-call(s32[1]{0:T(128)} %bitcast.refs_0_, bf16[512,1024]{1,0:T(8,128)(2,1)} %refs_1_.3, f32[512,1024]{1,0:T(8,128)} %shard_map.189.refs_2_, bf16[4,32,1024]{2,1,0:T(8,128)(2,1)} %copy-done, bf16[4,32,1024]{2,1,0:T(8,128)(2,1)} %copy-done.7, ...), custom_call_target="tpu_custom_call" | custom-call | tf_op jit(solution)/shard_map/pallas_call | solution.py:115
  41.8 0.9 collective-permute-start.13
  42.8 1.1 collective-permute-start.14
  43.9 1.4 collective-permute-start.15
  45.6 5.5 %collective-permute-done.13.refs_7_ = bf16[4,32,1024]{2,1,0:T(8,128)(2,1)} collective-permute-done((bf16[4,32,1024]{2,1,0:T(8,128)(2,1)S(1)}, bf16[4,32,1024]{2,1,0:T(8,128)(2,1)}, u32[]{:S(2)}, u32[]{:S(2)}) %collective-permute-start.13) | collective-permute-done | bytes 262176 | tf_op jit(solution)/shard_map/ppermute | solution.py:44
  51.1 4.4 %collective-permute-done.14.refs_8_ = bf16[4,32,1024]{2,1,0:T(8,128)(2,1)} collective-permute-done((bf16[4,32,1024]{2,1,0:T(8,128)(2,1)S(1)}, bf16[4,32,1024]{2,1,0:T(8,128)(2,1)}, u32[]{:S(2)}, u32[]{:S(2)}) %collective-permute-start.14) | collective-permute-done | bytes 262176 | tf_op jit(solution)/shard_map/ppermute | solution.py:44
  55.5 1.7 %collective-permute-done.15.refs_9_ = bf16[4,32,1024]{2,1,0:T(8,128)(2,1)} collective-permute-done((bf16[4,32,1024]{2,1,0:T(8,128)(2,1)S(1)}, bf16[4,32,1024]{2,1,0:T(8,128)(2,1)}, u32[]{:S(2)}, u32[]{:S(2)}) %collective-permute-start.15) | collective-permute-done | bytes 262176 | tf_op jit(solution)/shard_map/ppermute | solution.py:44
  57.2 2.0 %fusion.28 = (bf16[16,32,1024]{2,1,0:T(8,128)(2,1)S(1)}, f32[16,32,1024]{2,1,0:T(8,128)S(1)}) fusion(f32[16,32,1024]{2,1,0:T(8,128)} %get-tuple-element.34, bf16[16,32,1024]{2,1,0:T(8,128)(2,1)S(1)} %collective-permute-done.20), kind=kLoop, calls=%fused_computation.51 | loop fusion | flops 1572864 | bytes 6291456 | tf_op jit(solution)/shard_map/convert.12
  59.3 1.4 collective-permute-start.21
  60.7 1.5 collective-permute-start.22
  62.2 0.7 copy-done.18
  62.9 0.7 collective-permute-start.23
  63.6 11.4 %all_to_all.22 = f32[32,1,68]{2,1,0:T(1,128)S(1)} all-to-all(f32[32,1,68]{2,1,0:T(1,128)S(1)} %bitcast.39), channel_id=1, replica_groups=mesh['dev'=32] {'dev'}, dimensions={0} | all-to-all | bytes 17408 | tf_op jit(solution)/shard_map/all_to_all | solution.py:95
  75.1 0.7 reshape.105.refs_3_
  75.9 12.3 %shard_map.191 = (f32[256,128]{1,0:T(8,128)}, f32[16,32,1024]{2,1,0:T(8,128)}, bf16[16,32,1024]{2,1,0:T(8,128)(2,1)}) custom-call(s32[1]{0:T(128)} %bitcast.refs_0_, bf16[512,1024]{1,0:T(8,128)(2,1)} %refs_1_.3, f32[512,1024]{1,0:T(8,128)} %shard_map.189.refs_2_, f32[2,1024]{1,0:T(2,128)} %reshape.105.refs_3_, s32[8,512]{1,0:T(8,128)} %bitcast.38, ...), custom_call_target="tpu_custom_call" | custom-call | tf_op jit(solution)/shard_map/pallas_call | solution.py:115
  88.3 1.3 fusion.26
  89.6 0.8 collective-permute-start.24
  90.5 1.8 %collective-permute-start.25 = (bf16[1,32,1024]{2,1,0:T(8,128)(2,1)S(1)}, bf16[1,32,1024]{2,1,0:T(8,128)(2,1)S(1)}, u32[]{:S(2)}, u32[]{:S(2)}) collective-permute-start(bf16[1,32,1024]{2,1,0:T(8,128)(2,1)S(1)} %get-tuple-element.70), channel_id=1, source_target_pairs={{0,16},{1,17},{2,18},{3,19},{4,20},{5,21},{6,22},{7,23},{8,24},{9,... | collective-permute-start | bytes 196616 | tf_op jit(solution)/shard_map/ppermute | solution.py:44
  92.2 1.9 %collective-permute-start.26 = (bf16[1,32,1024]{2,1,0:T(8,128)(2,1)S(1)}, bf16[1,32,1024]{2,1,0:T(8,128)(2,1)S(1)}, u32[]{:S(2)}, u32[]{:S(2)}) collective-permute-start(bf16[1,32,1024]{2,1,0:T(8,128)(2,1)S(1)} %get-tuple-element.69), channel_id=1, source_target_pairs={{0,24},{1,25},{2,26},{3,27},{4,28},{5,29},{6,30},{7,31},{8,16},{9,... | collective-permute-start | bytes 196616 | tf_op jit(solution)/shard_map/ppermute | solution.py:44
  94.2 4.8 %collective-permute-done.25 = bf16[1,32,1024]{2,1,0:T(8,128)(2,1)S(1)} collective-permute-done((bf16[1,32,1024]{2,1,0:T(8,128)(2,1)S(1)}, bf16[1,32,1024]{2,1,0:T(8,128)(2,1)S(1)}, u32[]{:S(2)}, u32[]{:S(2)}) %collective-permute-start.25) | collective-permute-done | bytes 65568 | tf_op jit(solution)/shard_map/ppermute | solution.py:44
  99.1 1.3 collective-permute-start.27
  100.4 1.0 collective-permute-start.28
  101.4 2.1 %collective-permute-start.29 = (bf16[1,32,1024]{2,1,0:T(8,128)(2,1)S(1)}, bf16[1,32,1024]{2,1,0:T(8,128)(2,1)S(1)}, u32[]{:S(2)}, u32[]{:S(2)}) collective-permute-start(bf16[1,32,1024]{2,1,0:T(8,128)(2,1)S(1)} %get-tuple-element.53), channel_id=1, source_target_pairs={{0,24},{1,25},{2,26},{3,27},{4,28},{5,29},{6,30},{7,31},{8,16},{9,... | collective-permute-start | bytes 196616 | tf_op jit(solution)/shard_map/ppermute | solution.py:44
  103.6 3.0 %all-to-all-start.1 = ((f32[32,8,128]{2,1,0:T(8,128)}), f32[32,8,128]{2,1,0:T(8,128)S(1)}, u32[]{:S(2)}, u32[]{:S(2)}) async-start(f32[32,8,128]{2,1,0:T(8,128)} %bitcast.9), calls=%async_computation.1 | async-start | bytes 262144 | tf_op jit(solution)/shard_map/all_to_all | solution.py:95
  106.8 0.8 collective-permute-done.29
  107.7 1.6 %collective-permute-start.30 = (bf16[4,32,1024]{2,1,0:T(8,128)(2,1)S(1)}, bf16[4,32,1024]{2,1,0:T(8,128)(2,1)}, u32[]{:S(2)}, u32[]{:S(2)}) collective-permute-start(bf16[4,32,1024]{2,1,0:T(8,128)(2,1)S(1)} %pad_maximum_fusion.2.refs_3_), channel_id=1, source_target_pairs={{0,2},{1,3},{2,0},{3,1},{4,6},{5,7},{6,4},{7,5},{8,10},{9,11},{10,... | collective-permute-start | bytes 786440 | tf_op jit(solution)/shard_map/ppermute | solution.py:44
  109.3 0.8 collective-permute-start.31
  110.1 1.1 collective-permute-start.32
  111.2 2.3 %fusion.23 = (bf16[16,32,1024]{2,1,0:T(8,128)(2,1)S(1)}, f32[16,32,1024]{2,1,0:T(8,128)S(1)}) fusion(f32[16,32,1024]{2,1,0:T(8,128)} %get-tuple-element.44, bf16[16,32,1024]{2,1,0:T(8,128)(2,1)} %collective-permute-done.37), kind=kLoop, calls=%fused_computation.48 | loop fusion | flops 1572864 | bytes 6291456 | tf_op jit(solution)/shard_map/convert.6
  113.5 0.8 fusion.29
  114.4 1.6 %collective-permute-start.38 = (bf16[4,32,1024]{2,1,0:T(8,128)(2,1)}, bf16[4,32,1024]{2,1,0:T(8,128)(2,1)}, u32[]{:S(2)}, u32[]{:S(2)}) collective-permute-start(bf16[4,32,1024]{2,1,0:T(8,128)(2,1)} %get-tuple-element.46), channel_id=1, source_target_pairs={{0,2},{1,3},{2,0},{3,1},{4,6},{5,7},{6,4},{7,5},{8,10},{9,11},{10,... | collective-permute-start | bytes 786440 | tf_op jit(solution)/shard_map/ppermute | solution.py:44
  116.0 0.8 collective-permute-start.39
  116.8 0.9 collective-permute-done.30.refs_4_
  117.7 1.7 %collective-permute-start.40 = (bf16[4,32,1024]{2,1,0:T(8,128)(2,1)S(1)}, bf16[4,32,1024]{2,1,0:T(8,128)(2,1)S(1)}, u32[]{:S(2)}, u32[]{:S(2)}) collective-permute-start(bf16[4,32,1024]{2,1,0:T(8,128)(2,1)S(1)} %get-tuple-element.48), channel_id=1, source_target_pairs={{0,6},{1,7},{2,4},{3,5},{4,2},{5,3},{6,0},{7,1},{8,14},{9,15},{10,... | collective-permute-start | bytes 786440 | tf_op jit(solution)/shard_map/ppermute | solution.py:44
  120.3 0.7 reshape.111.refs_1_
  121.6 0.7 reshape.103.refs_1_
  122.9 1.9 %shard_map.192 = (f32[64,128]{1,0:T(8,128)}, f32[64,128]{1,0:T(8,128)}, f32[256,128]{1,0:T(8,128)}, f32[1,128]{1,0:T(1,128)}) custom-call(s32[1]{0:T(128)} %bitcast.refs_0_, s32[1,256]{1,0:T(1,128)} %reshape.103.refs_1_, f32[256,128]{1,0:T(8,128)} %bitcast.21, f32[64,128]{1,0:T(8,128)} %refs_3_.2, f32[64,128]{1,0:T(8,128)} %refs_4_.2, f32[1,128]{1,0:T(1,128)} %pad.13.refs_5_), custom_call_target="tpu_custom_call" | custom-call | tf_op jit(solution)/shard_map/pallas_call | solution.py:115
  124.9 3.6 %all-to-all-start.2 = ((f32[32,8,128]{2,1,0:T(8,128)}), f32[32,8,128]{2,1,0:T(8,128)S(1)}, u32[]{:S(2)}, u32[]{:S(2)}) async-start(f32[32,8,128]{2,1,0:T(8,128)} %bitcast.36), calls=%async_computation.2 | async-start | bytes 262144 | tf_op jit(solution)/shard_map/all_to_all | solution.py:95
  129.2 5.3 %collective-permute-done.39 = bf16[4,32,1024]{2,1,0:T(8,128)(2,1)} collective-permute-done((bf16[4,32,1024]{2,1,0:T(8,128)(2,1)}, bf16[4,32,1024]{2,1,0:T(8,128)(2,1)}, u32[]{:S(2)}, u32[]{:S(2)}) %collective-permute-start.39) | collective-permute-done | bytes 262176 | tf_op jit(solution)/shard_map/ppermute | solution.py:44
  134.5 1.0 collective-permute-done.40
  135.5 0.7 copy-done.19
  136.2 1.2 fusion.1
  137.5 1.6 %collective-permute-start.41 = (bf16[1,32,1024]{2,1,0:T(8,128)(2,1)S(1)}, bf16[1,32,1024]{2,1,0:T(8,128)(2,1)S(1)}, u32[]{:S(2)}, u32[]{:S(2)}) collective-permute-start(bf16[1,32,1024]{2,1,0:T(8,128)(2,1)S(1)} %get-tuple-element.65), channel_id=1, source_target_pairs={{0,8},{1,9},{2,10},{3,11},{4,12},{5,13},{6,14},{7,15},{8,0},{9,1},... | collective-permute-start | bytes 196616 | tf_op jit(solution)/shard_map/ppermute | solution.py:44
  139.0 0.7 copy-done.17
  139.7 2.5 %collective-permute-start.42 = (bf16[1,32,1024]{2,1,0:T(8,128)(2,1)S(1)}, bf16[1,32,1024]{2,1,0:T(8,128)(2,1)S(1)}, u32[]{:S(2)}, u32[]{:S(2)}) collective-permute-start(bf16[1,32,1024]{2,1,0:T(8,128)(2,1)S(1)} %get-tuple-element.67), channel_id=1, source_target_pairs={{0,16},{1,17},{2,18},{3,19},{4,20},{5,21},{6,22},{7,23},{8,24},{9,... | collective-permute-start | bytes 196616 | tf_op jit(solution)/shard_map/ppermute | solution.py:44
  143.3 2.7 %shard_map.195 = (f32[1024,128]{1,0:T(8,128)}, f32[1024,128]{1,0:T(8,128)}) custom-call(s32[1]{0:T(128)} %bitcast.refs_0_, s32[1,256]{1,0:T(1,128)} %reshape.111.refs_1_, f32[256,128]{1,0:T(8,128)} %bitcast.22, f32[1024,128]{1,0:T(8,128)} %refs_3_.3, f32[1024,128]{1,0:T(8,128)} %refs_4_.3), custom_call_target="tpu_custom_call" | custom-call | tf_op jit(solution)/shard_map/pallas_call | solution.py:115
  146.6 3.0 %shard_map.193 = (f32[512,1024]{1,0:T(8,128)}, f32[1,1024]{1,0:T(1,128)}) custom-call(s32[1]{0:T(128)} %bitcast.refs_0_, s32[8,512]{1,0:T(8,128)} %fusion.17.refs_1_, f32[256,128]{1,0:T(8,128)} %bitcast.26), custom_call_target="tpu_custom_call" | custom-call | tf_op jit(solution)/shard_map/pallas_call | solution.py:115
  149.6 4.6 %shard_map.194 = bf16[512,1024]{1,0:T(8,128)(2,1)} custom-call(s32[1]{0:T(128)} %bitcast.refs_0_, f32[512,1024]{1,0:T(8,128)} %get-tuple-element.38.refs_1_, f32[1,1024]{1,0:T(1,128)} %get-tuple-element.39.refs_2_, bf16[4,32,1024]{2,1,0:T(8,128)(2,1)} %copy-done.2, bf16[4,32,1024]{2,1,0:T(8,128)(2,1)} %collective-permute-done.30.refs_4_, ...), custom_call_target="tpu_custom_call" | custom-call | tf_op jit(solution)/shard_map/pallas_call | solution.py:115
  154.4 0.7 maximum_bitcast_fusion
  (128 shorter events, 8.3 us)
Async XLA Ops:
  1.6 5.7 %collective-permute-start = (bf16[1,32,1024]{2,1,0:T(8,128)(2,1)S(1)}, bf16[1,32,1024]{2,1,0:T(8,128)(2,1)S(1)}, u32[]{:S(2)}, u32[]{:S(2)}) collective-permute-start(bf16[1,32,1024]{2,1,0:T(8,128)(2,1)S(1)} %get-tuple-element.72), channel_id=1, source_target_pairs={{0,8},{1,9},{2,10},{3,11},{4,12},{5,13},{6,14},{7,15},{8,0},{9,1},... | collective-permute-start | bytes 196616 | tf_op jit(solution)/shard_map/ppermute | solution.py:44
  4.7 7.3 %collective-permute-start.1 = (bf16[1,32,1024]{2,1,0:T(8,128)(2,1)S(1)}, bf16[1,32,1024]{2,1,0:T(8,128)(2,1)S(1)}, u32[]{:S(2)}, u32[]{:S(2)}) collective-permute-start(bf16[1,32,1024]{2,1,0:T(8,128)(2,1)S(1)} %get-tuple-element.72), channel_id=1, source_target_pairs={{0,16},{1,17},{2,18},{3,19},{4,20},{5,21},{6,22},{7,23},{8,24},{9,... | collective-permute-start | bytes 196616 | tf_op jit(solution)/shard_map/ppermute | solution.py:44
  7.3 6.1 %collective-permute-start.2 = (bf16[1,32,1024]{2,1,0:T(8,128)(2,1)S(1)}, bf16[1,32,1024]{2,1,0:T(8,128)(2,1)S(1)}, u32[]{:S(2)}, u32[]{:S(2)}) collective-permute-start(bf16[1,32,1024]{2,1,0:T(8,128)(2,1)S(1)} %get-tuple-element.72), channel_id=1, source_target_pairs={{0,24},{1,25},{2,26},{3,27},{4,28},{5,29},{6,30},{7,31},{8,16},{9,... | collective-permute-start | bytes 196616 | tf_op jit(solution)/shard_map/ppermute | solution.py:44
  13.4 20.1 %copy-start = (bf16[4,32,1024]{2,1,0:T(8,128)(2,1)}, bf16[4,32,1024]{2,1,0:T(8,128)(2,1)S(1)}, u32[]{:S(2)}) copy-start(bf16[4,32,1024]{2,1,0:T(8,128)(2,1)S(1)} %pad_maximum_fusion.refs_3_.refs_14_) | copy-start | bytes 786436
  13.5 9.2 %collective-permute-start.6 = (bf16[4,32,1024]{2,1,0:T(8,128)(2,1)S(1)}, bf16[4,32,1024]{2,1,0:T(8,128)(2,1)S(1)}, u32[]{:S(2)}, u32[]{:S(2)}) collective-permute-start(bf16[4,32,1024]{2,1,0:T(8,128)(2,1)S(1)} %pad_maximum_fusion.refs_3_.refs_14_), channel_id=1, source_target_pairs={{0,2},{1,3},{2,0},{3,1},{4,6},{5,7},{6,4},{7,5},{8,10},{9,11},{10,... | collective-permute-start | bytes 786440 | tf_op jit(solution)/shard_map/ppermute | solution.py:44
  15.0 11.8 %collective-permute-start.7 = (bf16[4,32,1024]{2,1,0:T(8,128)(2,1)S(1)}, bf16[4,32,1024]{2,1,0:T(8,128)(2,1)S(1)}, u32[]{:S(2)}, u32[]{:S(2)}) collective-permute-start(bf16[4,32,1024]{2,1,0:T(8,128)(2,1)S(1)} %pad_maximum_fusion.refs_3_.refs_14_), channel_id=1, source_target_pairs={{0,4},{1,5},{2,6},{3,7},{4,0},{5,1},{6,2},{7,3},{8,12},{9,13},{10,... | collective-permute-start | bytes 786440 | tf_op jit(solution)/shard_map/ppermute | solution.py:44
  16.5 10.3 %collective-permute-start.8 = (bf16[4,32,1024]{2,1,0:T(8,128)(2,1)S(1)}, bf16[4,32,1024]{2,1,0:T(8,128)(2,1)S(1)}, u32[]{:S(2)}, u32[]{:S(2)}) collective-permute-start(bf16[4,32,1024]{2,1,0:T(8,128)(2,1)S(1)} %pad_maximum_fusion.refs_3_.refs_14_), channel_id=1, source_target_pairs={{0,6},{1,7},{2,4},{3,5},{4,2},{5,3},{6,0},{7,1},{8,14},{9,15},{10,... | collective-permute-start | bytes 786440 | tf_op jit(solution)/shard_map/ppermute | solution.py:44
  17.0 4.3 %collective-permute-start.3 = (bf16[1,32,1024]{2,1,0:T(8,128)(2,1)S(1)}, bf16[1,32,1024]{2,1,0:T(8,128)(2,1)S(1)}, u32[]{:S(2)}, u32[]{:S(2)}) collective-permute-start(bf16[1,32,1024]{2,1,0:T(8,128)(2,1)S(1)} %bitcast.29), channel_id=1, source_target_pairs={{0,8},{1,9},{2,10},{3,11},{4,12},{5,13},{6,14},{7,15},{8,0},{9,1},... | collective-permute-start | bytes 196616 | tf_op jit(solution)/shard_map/ppermute | solution.py:44
  17.0 10.3 %collective-permute-start.4 = (bf16[1,32,1024]{2,1,0:T(8,128)(2,1)S(1)}, bf16[1,32,1024]{2,1,0:T(8,128)(2,1)S(1)}, u32[]{:S(2)}, u32[]{:S(2)}) collective-permute-start(bf16[1,32,1024]{2,1,0:T(8,128)(2,1)S(1)} %bitcast.30), channel_id=1, source_target_pairs={{0,16},{1,17},{2,18},{3,19},{4,20},{5,21},{6,22},{7,23},{8,24},{9,... | collective-permute-start | bytes 196616 | tf_op jit(solution)/shard_map/ppermute | solution.py:44
  21.3 12.2 %collective-permute-start.9 = (bf16[4,32,1024]{2,1,0:T(8,128)(2,1)S(1)}, bf16[4,32,1024]{2,1,0:T(8,128)(2,1)S(1)}, u32[]{:S(2)}, u32[]{:S(2)}) collective-permute-start(bf16[4,32,1024]{2,1,0:T(8,128)(2,1)S(1)} %pad_maximum_fusion.refs_3_.refs_14_), channel_id=1, source_target_pairs={{0,1},{1,0},{2,3},{3,2},{4,5},{5,4},{6,7},{7,6},{8,9},{9,8},{10,11... | collective-permute-start | bytes 786440 | tf_op jit(solution)/shard_map/ppermute | solution.py:44
  22.7 10.8 %copy-start.7 = (bf16[4,32,1024]{2,1,0:T(8,128)(2,1)}, bf16[4,32,1024]{2,1,0:T(8,128)(2,1)S(1)}, u32[]{:S(2)}) copy-start(bf16[4,32,1024]{2,1,0:T(8,128)(2,1)S(1)} %collective-permute-done.6.refs_4_.refs_15_) | copy-start | bytes 786436
  22.7 10.8 %collective-permute-start.10 = (bf16[4,32,1024]{2,1,0:T(8,128)(2,1)S(1)}, bf16[4,32,1024]{2,1,0:T(8,128)(2,1)S(1)}, u32[]{:S(2)}, u32[]{:S(2)}) collective-permute-start(bf16[4,32,1024]{2,1,0:T(8,128)(2,1)S(1)} %collective-permute-done.6.refs_4_.refs_15_), channel_id=1, source_target_pairs={{0,1},{1,0},{2,3},{3,2},{4,5},{5,4},{6,7},{7,6},{8,9},{9,8},{10,11... | collective-permute-start | bytes 786440 | tf_op jit(solution)/shard_map/ppermute | solution.py:44
  26.8 6.8 %copy-start.8 = (bf16[4,32,1024]{2,1,0:T(8,128)(2,1)}, bf16[4,32,1024]{2,1,0:T(8,128)(2,1)S(1)}, u32[]{:S(2)}) copy-start(bf16[4,32,1024]{2,1,0:T(8,128)(2,1)S(1)} %collective-permute-done.7.refs_5_.refs_16_) | copy-start | bytes 786436
  26.8 6.7 %collective-permute-start.11 = (bf16[4,32,1024]{2,1,0:T(8,128)(2,1)S(1)}, bf16[4,32,1024]{2,1,0:T(8,128)(2,1)S(1)}, u32[]{:S(2)}, u32[]{:S(2)}) collective-permute-start(bf16[4,32,1024]{2,1,0:T(8,128)(2,1)S(1)} %collective-permute-done.7.refs_5_.refs_16_), channel_id=1, source_target_pairs={{0,1},{1,0},{2,3},{3,2},{4,5},{5,4},{6,7},{7,6},{8,9},{9,8},{10,11... | collective-permute-start | bytes 786440 | tf_op jit(solution)/shard_map/ppermute | solution.py:44
  26.8 6.8 %copy-start.9 = (bf16[4,32,1024]{2,1,0:T(8,128)(2,1)}, bf16[4,32,1024]{2,1,0:T(8,128)(2,1)S(1)}, u32[]{:S(2)}) copy-start(bf16[4,32,1024]{2,1,0:T(8,128)(2,1)S(1)} %collective-permute-done.8.refs_6_.refs_17_) | copy-start | bytes 786436
  26.8 6.7 %collective-permute-start.12 = (bf16[4,32,1024]{2,1,0:T(8,128)(2,1)S(1)}, bf16[4,32,1024]{2,1,0:T(8,128)(2,1)S(1)}, u32[]{:S(2)}, u32[]{:S(2)}) collective-permute-start(bf16[4,32,1024]{2,1,0:T(8,128)(2,1)S(1)} %collective-permute-done.8.refs_6_.refs_17_), channel_id=1, source_target_pairs={{0,1},{1,0},{2,3},{3,2},{4,5},{5,4},{6,7},{7,6},{8,9},{9,8},{10,11... | collective-permute-start | bytes 786440 | tf_op jit(solution)/shard_map/ppermute | solution.py:44
  27.3 6.1 %collective-permute-start.5 = (bf16[1,32,1024]{2,1,0:T(8,128)(2,1)S(1)}, bf16[1,32,1024]{2,1,0:T(8,128)(2,1)S(1)}, u32[]{:S(2)}, u32[]{:S(2)}) collective-permute-start(bf16[1,32,1024]{2,1,0:T(8,128)(2,1)S(1)} %bitcast.31), channel_id=1, source_target_pairs={{0,24},{1,25},{2,26},{3,27},{4,28},{5,29},{6,30},{7,31},{8,16},{9,... | collective-permute-start | bytes 196616 | tf_op jit(solution)/shard_map/ppermute | solution.py:44
  33.4 12.2 %copy-start.3 = (bf16[4,32,1024]{2,1,0:T(8,128)(2,1)}, bf16[4,32,1024]{2,1,0:T(8,128)(2,1)S(1)}, u32[]{:S(2)}) copy-start(bf16[4,32,1024]{2,1,0:T(8,128)(2,1)S(1)} %pad_maximum_fusion.1.refs_6_) | copy-start | bytes 786436
  33.4 11.9 %copy-start.25 = (s32[128]{0:T(128)S(1)}, s32[128]{0:T(128)}, u32[]{:S(2)}) copy-start(s32[128]{0:T(128)} %param.17) | copy-start | bytes 1540
  33.4 12.0 %copy-start.24 = (f32[2,32]{1,0:T(2,128)S(1)}, f32[2,32]{1,0:T(2,128)}, u32[]{:S(2)}) copy-start(f32[2,32]{1,0:T(2,128)} %param.26) | copy-start | bytes 772
  41.8 15.4 %collective-permute-start.20 = (bf16[16,32,1024]{2,1,0:T(8,128)(2,1)}, bf16[16,32,1024]{2,1,0:T(8,128)(2,1)S(1)}, u32[]{:S(2)}, u32[]{:S(2)}) collective-permute-start(bf16[16,32,1024]{2,1,0:T(8,128)(2,1)} %get-tuple-element.35), channel_id=1, source_target_pairs={{0,1},{1,0},{2,3},{3,2},{4,5},{5,4},{6,7},{7,6},{8,9},{9,8},{10,11... | collective-permute-start | bytes 3145736 | tf_op jit(solution)/shard_map/ppermute | solution.py:44
  41.8 9.3 %collective-permute-start.13 = (bf16[4,32,1024]{2,1,0:T(8,128)(2,1)S(1)}, bf16[4,32,1024]{2,1,0:T(8,128)(2,1)}, u32[]{:S(2)}, u32[]{:S(2)}) collective-permute-start(bf16[4,32,1024]{2,1,0:T(8,128)(2,1)S(1)} %pad_maximum_fusion.1.refs_6_), channel_id=1, source_target_pairs={{0,2},{1,3},{2,0},{3,1},{4,6},{5,7},{6,4},{7,5},{8,10},{9,11},{10,... | collective-permute-start | bytes 786440 | tf_op jit(solution)/shard_map/ppermute | solution.py:44
  42.8 12.7 %collective-permute-start.14 = (bf16[4,32,1024]{2,1,0:T(8,128)(2,1)S(1)}, bf16[4,32,1024]{2,1,0:T(8,128)(2,1)}, u32[]{:S(2)}, u32[]{:S(2)}) collective-permute-start(bf16[4,32,1024]{2,1,0:T(8,128)(2,1)S(1)} %pad_maximum_fusion.1.refs_6_), channel_id=1, source_target_pairs={{0,4},{1,5},{2,6},{3,7},{4,0},{5,1},{6,2},{7,3},{8,12},{9,13},{10,... | collective-permute-start | bytes 786440 | tf_op jit(solution)/shard_map/ppermute | solution.py:44
  43.9 13.3 %collective-permute-start.15 = (bf16[4,32,1024]{2,1,0:T(8,128)(2,1)S(1)}, bf16[4,32,1024]{2,1,0:T(8,128)(2,1)}, u32[]{:S(2)}, u32[]{:S(2)}) collective-permute-start(bf16[4,32,1024]{2,1,0:T(8,128)(2,1)S(1)} %pad_maximum_fusion.1.refs_6_), channel_id=1, source_target_pairs={{0,6},{1,7},{2,4},{3,5},{4,2},{5,3},{6,0},{7,1},{8,14},{9,15},{10,... | collective-permute-start | bytes 786440 | tf_op jit(solution)/shard_map/ppermute | solution.py:44
  45.6 15.1 %collective-permute-start.16 = (bf16[4,32,1024]{2,1,0:T(8,128)(2,1)S(1)}, bf16[4,32,1024]{2,1,0:T(8,128)(2,1)S(1)}, u32[]{:S(2)}, u32[]{:S(2)}) collective-permute-start(bf16[4,32,1024]{2,1,0:T(8,128)(2,1)S(1)} %pad_maximum_fusion.1.refs_6_), channel_id=1, source_target_pairs={{0,1},{1,0},{2,3},{3,2},{4,5},{5,4},{6,7},{7,6},{8,9},{9,8},{10,11... | collective-permute-start | bytes 786440 | tf_op jit(solution)/shard_map/ppermute | solution.py:44
  51.1 11.1 %collective-permute-start.17 = (bf16[4,32,1024]{2,1,0:T(8,128)(2,1)}, bf16[4,32,1024]{2,1,0:T(8,128)(2,1)S(1)}, u32[]{:S(2)}, u32[]{:S(2)}) collective-permute-start(bf16[4,32,1024]{2,1,0:T(8,128)(2,1)} %collective-permute-done.13.refs_7_), channel_id=1, source_target_pairs={{0,1},{1,0},{2,3},{3,2},{4,5},{5,4},{6,7},{7,6},{8,9},{9,8},{10,11... | collective-permute-start | bytes 786440 | tf_op jit(solution)/shard_map/ppermute | solution.py:44
  55.5 20.4 %collective-permute-start.18 = (bf16[4,32,1024]{2,1,0:T(8,128)(2,1)}, bf16[4,32,1024]{2,1,0:T(8,128)(2,1)}, u32[]{:S(2)}, u32[]{:S(2)}) collective-permute-start(bf16[4,32,1024]{2,1,0:T(8,128)(2,1)} %collective-permute-done.14.refs_8_), channel_id=1, source_target_pairs={{0,1},{1,0},{2,3},{3,2},{4,5},{5,4},{6,7},{7,6},{8,9},{9,8},{10,11... | collective-permute-start | bytes 786440 | tf_op jit(solution)/shard_map/ppermute | solution.py:44
  57.2 18.6 %collective-permute-start.19 = (bf16[4,32,1024]{2,1,0:T(8,128)(2,1)}, bf16[4,32,1024]{2,1,0:T(8,128)(2,1)}, u32[]{:S(2)}, u32[]{:S(2)}) collective-permute-start(bf16[4,32,1024]{2,1,0:T(8,128)(2,1)} %collective-permute-done.15.refs_9_), channel_id=1, source_target_pairs={{0,1},{1,0},{2,3},{3,2},{4,5},{5,4},{6,7},{7,6},{8,9},{9,8},{10,11... | collective-permute-start | bytes 786440 | tf_op jit(solution)/shard_map/ppermute | solution.py:44
  59.3 16.5 %copy-start.4 = (bf16[4,32,1024]{2,1,0:T(8,128)(2,1)}, bf16[4,32,1024]{2,1,0:T(8,128)(2,1)S(1)}, u32[]{:S(2)}) copy-start(bf16[4,32,1024]{2,1,0:T(8,128)(2,1)S(1)} %get-tuple-element.62.refs_24_) | copy-start | bytes 786436
  59.3 16.5 %copy-start.5 = (bf16[4,32,1024]{2,1,0:T(8,128)(2,1)}, bf16[4,32,1024]{2,1,0:T(8,128)(2,1)S(1)}, u32[]{:S(2)}) copy-start(bf16[4,32,1024]{2,1,0:T(8,128)(2,1)S(1)} %get-tuple-element.63.refs_23_) | copy-start | bytes 786436
  59.3 16.5 %copy-start.6 = (bf16[4,32,1024]{2,1,0:T(8,128)(2,1)}, bf16[4,32,1024]{2,1,0:T(8,128)(2,1)S(1)}, u32[]{:S(2)}) copy-start(bf16[4,32,1024]{2,1,0:T(8,128)(2,1)S(1)} %get-tuple-element.64.refs_22_) | copy-start | bytes 786436
  59.3 29.0 %collective-permute-start.21 = (bf16[4,32,1024]{2,1,0:T(8,128)(2,1)S(1)}, bf16[4,32,1024]{2,1,0:T(8,128)(2,1)}, u32[]{:S(2)}, u32[]{:S(2)}) collective-permute-start(bf16[4,32,1024]{2,1,0:T(8,128)(2,1)S(1)} %get-tuple-element.64.refs_22_), channel_id=1, source_target_pairs={{0,2},{1,3},{2,0},{3,1},{4,6},{5,7},{6,4},{7,5},{8,10},{9,11},{10,... | collective-permute-start | bytes 786440 | tf_op jit(solution)/shard_map/ppermute | solution.py:44
  60.7 1.5 copy-start.16
  60.7 27.6 %collective-permute-start.22 = (bf16[4,32,1024]{2,1,0:T(8,128)(2,1)S(1)}, bf16[4,32,1024]{2,1,0:T(8,128)(2,1)}, u32[]{:S(2)}, u32[]{:S(2)}) collective-permute-start(bf16[4,32,1024]{2,1,0:T(8,128)(2,1)S(1)} %get-tuple-element.63.refs_23_), channel_id=1, source_target_pairs={{0,4},{1,5},{2,6},{3,7},{4,0},{5,1},{6,2},{7,3},{8,12},{9,13},{10,... | collective-permute-start | bytes 786440 | tf_op jit(solution)/shard_map/ppermute | solution.py:44
  62.9 25.4 %collective-permute-start.23 = (bf16[4,32,1024]{2,1,0:T(8,128)(2,1)S(1)}, bf16[4,32,1024]{2,1,0:T(8,128)(2,1)}, u32[]{:S(2)}, u32[]{:S(2)}) collective-permute-start(bf16[4,32,1024]{2,1,0:T(8,128)(2,1)S(1)} %get-tuple-element.62.refs_24_), channel_id=1, source_target_pairs={{0,6},{1,7},{2,4},{3,5},{4,2},{5,3},{6,0},{7,1},{8,14},{9,15},{10,... | collective-permute-start | bytes 786440 | tf_op jit(solution)/shard_map/ppermute | solution.py:44
  88.2 10.8 %copy-start.14 = (f32[2,1024,32]{1,2,0:T(8,128)S(1)}, f32[2,1024,32]{1,2,0:T(8,128)}, u32[]{:S(2)}) copy-start(f32[2,1024,32]{1,2,0:T(8,128)} %param.25) | copy-start | bytes 786436
  88.2 10.8 %copy-start.20 = (f32[2,1024,32]{1,2,0:T(8,128)S(1)}, f32[2,1024,32]{1,2,0:T(8,128)}, u32[]{:S(2)}) copy-start(f32[2,1024,32]{1,2,0:T(8,128)} %param.27) | copy-start | bytes 786436
  88.2 23.0 %collective-permute-start.37 = (bf16[16,32,1024]{2,1,0:T(8,128)(2,1)}, bf16[16,32,1024]{2,1,0:T(8,128)(2,1)}, u32[]{:S(2)}, u32[]{:S(2)}) collective-permute-start(bf16[16,32,1024]{2,1,0:T(8,128)(2,1)} %get-tuple-element.45), channel_id=1, source_target_pairs={{0,1},{1,0},{2,3},{3,2},{4,5},{5,4},{6,7},{7,6},{8,9},{9,8},{10,11... | collective-permute-start | bytes 3145736 | tf_op jit(solution)/shard_map/ppermute | solution.py:44
  89.6 4.5 %collective-permute-start.24 = (bf16[1,32,1024]{2,1,0:T(8,128)(2,1)S(1)}, bf16[1,32,1024]{2,1,0:T(8,128)(2,1)S(1)}, u32[]{:S(2)}, u32[]{:S(2)}) collective-permute-start(bf16[1,32,1024]{2,1,0:T(8,128)(2,1)S(1)} %get-tuple-element.68), channel_id=1, source_target_pairs={{0,8},{1,9},{2,10},{3,11},{4,12},{5,13},{6,14},{7,15},{8,0},{9,1},... | collective-permute-start | bytes 196616 | tf_op jit(solution)/shard_map/ppermute | solution.py:44
  90.5 8.5 %collective-permute-start.25 = (bf16[1,32,1024]{2,1,0:T(8,128)(2,1)S(1)}, bf16[1,32,1024]{2,1,0:T(8,128)(2,1)S(1)}, u32[]{:S(2)}, u32[]{:S(2)}) collective-permute-start(bf16[1,32,1024]{2,1,0:T(8,128)(2,1)S(1)} %get-tuple-element.70), channel_id=1, source_target_pairs={{0,16},{1,17},{2,18},{3,19},{4,20},{5,21},{6,22},{7,23},{8,24},{9,... | collective-permute-start | bytes 196616 | tf_op jit(solution)/shard_map/ppermute | solution.py:44
  92.2 6.8 %collective-permute-start.26 = (bf16[1,32,1024]{2,1,0:T(8,128)(2,1)S(1)}, bf16[1,32,1024]{2,1,0:T(8,128)(2,1)S(1)}, u32[]{:S(2)}, u32[]{:S(2)}) collective-permute-start(bf16[1,32,1024]{2,1,0:T(8,128)(2,1)S(1)} %get-tuple-element.69), channel_id=1, source_target_pairs={{0,24},{1,25},{2,26},{3,27},{4,28},{5,29},{6,30},{7,31},{8,16},{9,... | collective-permute-start | bytes 196616 | tf_op jit(solution)/shard_map/ppermute | solution.py:44
  99.1 7.5 %collective-permute-start.27 = (bf16[1,32,1024]{2,1,0:T(8,128)(2,1)S(1)}, bf16[1,32,1024]{2,1,0:T(8,128)(2,1)S(1)}, u32[]{:S(2)}, u32[]{:S(2)}) collective-permute-start(bf16[1,32,1024]{2,1,0:T(8,128)(2,1)S(1)} %get-tuple-element.53), channel_id=1, source_target_pairs={{0,8},{1,9},{2,10},{3,11},{4,12},{5,13},{6,14},{7,15},{8,0},{9,1},... | collective-permute-start | bytes 196616 | tf_op jit(solution)/shard_map/ppermute | solution.py:44
  100.4 6.4 %collective-permute-start.28 = (bf16[1,32,1024]{2,1,0:T(8,128)(2,1)S(1)}, bf16[1,32,1024]{2,1,0:T(8,128)(2,1)S(1)}, u32[]{:S(2)}, u32[]{:S(2)}) collective-permute-start(bf16[1,32,1024]{2,1,0:T(8,128)(2,1)S(1)} %get-tuple-element.53), channel_id=1, source_target_pairs={{0,16},{1,17},{2,18},{3,19},{4,20},{5,21},{6,22},{7,23},{8,24},{9,... | collective-permute-start | bytes 196616 | tf_op jit(solution)/shard_map/ppermute | solution.py:44
  101.4 6.2 %collective-permute-start.29 = (bf16[1,32,1024]{2,1,0:T(8,128)(2,1)S(1)}, bf16[1,32,1024]{2,1,0:T(8,128)(2,1)S(1)}, u32[]{:S(2)}, u32[]{:S(2)}) collective-permute-start(bf16[1,32,1024]{2,1,0:T(8,128)(2,1)S(1)} %get-tuple-element.53), channel_id=1, source_target_pairs={{0,24},{1,25},{2,26},{3,27},{4,28},{5,29},{6,30},{7,31},{8,16},{9,... | collective-permute-start | bytes 196616 | tf_op jit(solution)/shard_map/ppermute | solution.py:44
  103.6 18.7 %all-to-all-start.1 = ((f32[32,8,128]{2,1,0:T(8,128)}), f32[32,8,128]{2,1,0:T(8,128)S(1)}, u32[]{:S(2)}, u32[]{:S(2)}) async-start(f32[32,8,128]{2,1,0:T(8,128)} %bitcast.9), calls=%async_computation.1 | async-start | bytes 262144 | tf_op jit(solution)/shard_map/all_to_all | solution.py:95
  107.6 20.8 %copy-start.2 = (bf16[4,32,1024]{2,1,0:T(8,128)(2,1)}, bf16[4,32,1024]{2,1,0:T(8,128)(2,1)S(1)}, u32[]{:S(2)}) copy-start(bf16[4,32,1024]{2,1,0:T(8,128)(2,1)S(1)} %pad_maximum_fusion.2.refs_3_) | copy-start | bytes 786436
  107.7 10.1 %collective-permute-start.30 = (bf16[4,32,1024]{2,1,0:T(8,128)(2,1)S(1)}, bf16[4,32,1024]{2,1,0:T(8,128)(2,1)}, u32[]{:S(2)}, u32[]{:S(2)}) collective-permute-start(bf16[4,32,1024]{2,1,0:T(8,128)(2,1)S(1)} %pad_maximum_fusion.2.refs_3_), channel_id=1, source_target_pairs={{0,2},{1,3},{2,0},{3,1},{4,6},{5,7},{6,4},{7,5},{8,10},{9,11},{10,... | collective-permute-start | bytes 786440 | tf_op jit(solution)/shard_map/ppermute | solution.py:44
  109.3 19.2 %collective-permute-start.31 = (bf16[4,32,1024]{2,1,0:T(8,128)(2,1)S(1)}, bf16[4,32,1024]{2,1,0:T(8,128)(2,1)}, u32[]{:S(2)}, u32[]{:S(2)}) collective-permute-start(bf16[4,32,1024]{2,1,0:T(8,128)(2,1)S(1)} %pad_maximum_fusion.2.refs_3_), channel_id=1, source_target_pairs={{0,4},{1,5},{2,6},{3,7},{4,0},{5,1},{6,2},{7,3},{8,12},{9,13},{10,... | collective-permute-start | bytes 786440 | tf_op jit(solution)/shard_map/ppermute | solution.py:44
  110.1 18.5 %collective-permute-start.32 = (bf16[4,32,1024]{2,1,0:T(8,128)(2,1)S(1)}, bf16[4,32,1024]{2,1,0:T(8,128)(2,1)}, u32[]{:S(2)}, u32[]{:S(2)}) collective-permute-start(bf16[4,32,1024]{2,1,0:T(8,128)(2,1)S(1)} %pad_maximum_fusion.2.refs_3_), channel_id=1, source_target_pairs={{0,6},{1,7},{2,4},{3,5},{4,2},{5,3},{6,0},{7,1},{8,14},{9,15},{10,... | collective-permute-start | bytes 786440 | tf_op jit(solution)/shard_map/ppermute | solution.py:44
  111.2 8.2 %copy-start.22 = (s32[512,8]{0,1:T(8,128)S(1)}, s32[512,8]{0,1:T(8,128)}, u32[]{:S(2)}) copy-start(s32[512,8]{0,1:T(8,128)} %param.16) | copy-start | bytes 49156
  111.2 8.9 %copy-start.23 = (s32[1,32,2]{1,2,0:T(2,128)S(1)}, s32[1,32,2]{1,2,0:T(2,128)}, u32[]{:S(2)}) copy-start(s32[1,32,2]{1,2,0:T(2,128)} %param.18) | copy-start | bytes 772
  114.4 14.7 %collective-permute-start.38 = (bf16[4,32,1024]{2,1,0:T(8,128)(2,1)}, bf16[4,32,1024]{2,1,0:T(8,128)(2,1)}, u32[]{:S(2)}, u32[]{:S(2)}) collective-permute-start(bf16[4,32,1024]{2,1,0:T(8,128)(2,1)} %get-tuple-element.46), channel_id=1, source_target_pairs={{0,2},{1,3},{2,0},{3,1},{4,6},{5,7},{6,4},{7,5},{8,10},{9,11},{10,... | collective-permute-start | bytes 786440 | tf_op jit(solution)/shard_map/ppermute | solution.py:44
  116.0 18.5 %collective-permute-start.39 = (bf16[4,32,1024]{2,1,0:T(8,128)(2,1)}, bf16[4,32,1024]{2,1,0:T(8,128)(2,1)}, u32[]{:S(2)}, u32[]{:S(2)}) collective-permute-start(bf16[4,32,1024]{2,1,0:T(8,128)(2,1)} %get-tuple-element.47), channel_id=1, source_target_pairs={{0,4},{1,5},{2,6},{3,7},{4,0},{5,1},{6,2},{7,3},{8,12},{9,13},{10,... | collective-permute-start | bytes 786440 | tf_op jit(solution)/shard_map/ppermute | solution.py:44
  117.7 17.7 %collective-permute-start.40 = (bf16[4,32,1024]{2,1,0:T(8,128)(2,1)S(1)}, bf16[4,32,1024]{2,1,0:T(8,128)(2,1)S(1)}, u32[]{:S(2)}, u32[]{:S(2)}) collective-permute-start(bf16[4,32,1024]{2,1,0:T(8,128)(2,1)S(1)} %get-tuple-element.48), channel_id=1, source_target_pairs={{0,6},{1,7},{2,4},{3,5},{4,2},{5,3},{6,0},{7,1},{8,14},{9,15},{10,... | collective-permute-start | bytes 786440 | tf_op jit(solution)/shard_map/ppermute | solution.py:44
  124.9 17.8 %copy-start.26 = (f32[1,128]{1,0:T(1,128)S(1)}, f32[1,128]{1,0:T(1,128)}, u32[]{:S(2)}) copy-start(f32[1,128]{1,0:T(1,128)} %get-tuple-element.50) | copy-start | bytes 1540
  124.9 21.1 %all-to-all-start.2 = ((f32[32,8,128]{2,1,0:T(8,128)}), f32[32,8,128]{2,1,0:T(8,128)S(1)}, u32[]{:S(2)}, u32[]{:S(2)}) async-start(f32[32,8,128]{2,1,0:T(8,128)} %bitcast.36), calls=%async_computation.2 | async-start | bytes 262144 | tf_op jit(solution)/shard_map/all_to_all | solution.py:95
  128.5 10.5 %collective-permute-start.33 = (bf16[4,32,1024]{2,1,0:T(8,128)(2,1)S(1)}, bf16[4,32,1024]{2,1,0:T(8,128)(2,1)S(1)}, u32[]{:S(2)}, u32[]{:S(2)}) collective-permute-start(bf16[4,32,1024]{2,1,0:T(8,128)(2,1)S(1)} %pad_maximum_fusion.2.refs_3_), channel_id=1, source_target_pairs={{0,1},{1,0},{2,3},{3,2},{4,5},{5,4},{6,7},{7,6},{8,9},{9,8},{10,11... | collective-permute-start | bytes 786440 | tf_op jit(solution)/shard_map/ppermute | solution.py:44
  128.6 13.6 %collective-permute-start.34 = (bf16[4,32,1024]{2,1,0:T(8,128)(2,1)}, bf16[4,32,1024]{2,1,0:T(8,128)(2,1)}, u32[]{:S(2)}, u32[]{:S(2)}) collective-permute-start(bf16[4,32,1024]{2,1,0:T(8,128)(2,1)} %collective-permute-done.30.refs_4_), channel_id=1, source_target_pairs={{0,1},{1,0},{2,3},{3,2},{4,5},{5,4},{6,7},{7,6},{8,9},{9,8},{10,11... | collective-permute-start | bytes 786440 | tf_op jit(solution)/shard_map/ppermute | solution.py:44
  129.1 20.5 %collective-permute-start.35 = (bf16[4,32,1024]{2,1,0:T(8,128)(2,1)}, bf16[4,32,1024]{2,1,0:T(8,128)(2,1)}, u32[]{:S(2)}, u32[]{:S(2)}) collective-permute-start(bf16[4,32,1024]{2,1,0:T(8,128)(2,1)} %collective-permute-done.31.refs_5_), channel_id=1, source_target_pairs={{0,1},{1,0},{2,3},{3,2},{4,5},{5,4},{6,7},{7,6},{8,9},{9,8},{10,11... | collective-permute-start | bytes 786440 | tf_op jit(solution)/shard_map/ppermute | solution.py:44
  134.5 15.1 %collective-permute-start.36 = (bf16[4,32,1024]{2,1,0:T(8,128)(2,1)}, bf16[4,32,1024]{2,1,0:T(8,128)(2,1)}, u32[]{:S(2)}, u32[]{:S(2)}) collective-permute-start(bf16[4,32,1024]{2,1,0:T(8,128)(2,1)} %collective-permute-done.32.refs_6_), channel_id=1, source_target_pairs={{0,1},{1,0},{2,3},{3,2},{4,5},{5,4},{6,7},{7,6},{8,9},{9,8},{10,11... | collective-permute-start | bytes 786440 | tf_op jit(solution)/shard_map/ppermute | solution.py:44
  137.5 16.8 %collective-permute-start.41 = (bf16[1,32,1024]{2,1,0:T(8,128)(2,1)S(1)}, bf16[1,32,1024]{2,1,0:T(8,128)(2,1)S(1)}, u32[]{:S(2)}, u32[]{:S(2)}) collective-permute-start(bf16[1,32,1024]{2,1,0:T(8,128)(2,1)S(1)} %get-tuple-element.65), channel_id=1, source_target_pairs={{0,8},{1,9},{2,10},{3,11},{4,12},{5,13},{6,14},{7,15},{8,0},{9,1},... | collective-permute-start | bytes 196616 | tf_op jit(solution)/shard_map/ppermute | solution.py:44
  139.7 14.5 %collective-permute-start.42 = (bf16[1,32,1024]{2,1,0:T(8,128)(2,1)S(1)}, bf16[1,32,1024]{2,1,0:T(8,128)(2,1)S(1)}, u32[]{:S(2)}, u32[]{:S(2)}) collective-permute-start(bf16[1,32,1024]{2,1,0:T(8,128)(2,1)S(1)} %get-tuple-element.67), channel_id=1, source_target_pairs={{0,16},{1,17},{2,18},{3,19},{4,20},{5,21},{6,22},{7,23},{8,24},{9,... | collective-permute-start | bytes 196616 | tf_op jit(solution)/shard_map/ppermute | solution.py:44
  142.2 12.0 %collective-permute-start.43 = (bf16[1,32,1024]{2,1,0:T(8,128)(2,1)S(1)}, bf16[1,32,1024]{2,1,0:T(8,128)(2,1)S(1)}, u32[]{:S(2)}, u32[]{:S(2)}) collective-permute-start(bf16[1,32,1024]{2,1,0:T(8,128)(2,1)S(1)} %get-tuple-element.66), channel_id=1, source_target_pairs={{0,24},{1,25},{2,26},{3,27},{4,28},{5,29},{6,30},{7,31},{8,16},{9,... | collective-permute-start | bytes 196616 | tf_op jit(solution)/shard_map/ppermute | solution.py:44
  149.6 4.6 %copy-start.21 = (f32[2,1024,32]{1,2,0:T(8,128)S(1)}, f32[2,1024,32]{1,2,0:T(8,128)}, u32[]{:S(2)}) copy-start(f32[2,1024,32]{1,2,0:T(8,128)} %param.27) | copy-start | bytes 786436
  (9 other events, 6.4 us)
where the time goes:
time: 156 us; the launch traced here: 155 us
  starting transfers between devices  48.6 us (31%)
  waiting for transfers between devices  38.8 us (25%)
  Pallas kernels  34.3 us (22%)
  blocking collectives  11.4 us (7%)
  local copies, waits for them, and re-layouts  10.9 us (7%)
  other arithmetic  10.1 us (6%)
    ppermute x44, starting transfers between devices, swap(): return lax.ppermute(values, 'dev', [(i, i ^ mask) for i in range(devices)])  42 us
    ppermute x44, waiting for transfers between devices, swap(): return lax.ppermute(values, 'dev', [(i, i ^ mask) for i in range(devices)])  38.8 us
    pallas_call x7, Pallas kernels, call(): pl.pallas_call(kernel, out_shape=[jax.ShapeDtypeStruct(*out) for out in o...  34.3 us
    all_to_all x1, blocking collectives, exchange(): lax.all_to_all(values, 'dev', split_axis=0, concat_axis=0, tiled=True)  11.4 us
    all_to_all x2, starting transfers between devices, exchange(): lax.all_to_all(values, 'dev', split_axis=0, concat_axis=0, tiled=True)  6.59 us
    another operation x4, other arithmetic  5.64 us
    unnamed x55, local copies, waits for them, and re-layouts  5.09 us
  transfers between devices with their start and end apart: 46, of which 16 were waited for; matrix products, arithmetic and copies ran while one was open for 9% of the time, Pallas kernels for 18%

commit v1 on v0

--- a/solution.py
+++ b/solution.py
@@ -143,17 +143,25 @@
     return [slice(at, at + step) for at in range(0, rows, step)]
 
 
-def pick(me, index, table, loose=()):
+def pick(me, index, shared, evicted):
     fields, samples = index.shape
-    rows, width = table.shape
-
-    def body(me_ref, index_ref, table_ref, out):
-        both = high_low(table_ref[...])
+    width = shared.shape[1]
+    rows = shared.shape[0] + evicted.shape[0]
+
+    def body(me_ref, index_ref, shared_ref, evicted_ref, out):
+        both = jnp.concatenate([high_low(shared_ref[...]), high_low(evicted_ref[...])], axis=0)
         for k in range(fields):
             picked = dot(one_hot(index_ref[k : k + 1, :], rows), both, 0, 0)
-            out[:, k * width : (k + 1) * width] = picked[:, :width] + picked[:, width:]
-
-    return call(body, [((samples, fields * width), f32)], [me, index, table], loose=loose)[0]
+            out[:, k * width : (k + 1) * width] = halves_sum(picked, width)
+
+    return call(body, [((samples, fields * width), f32)], [me, index, shared, evicted])[0]
+
+
+def pass_on(me, values):
+    def body(me_ref, values_ref, out):
+        out[...] = values_ref[...]
+
+    return call(body, [(values.shape, f32)], [me, values])[0]
 
 
 def step_two(me, masks, parts, upstream, feat):
@@ -239,9 +247,30 @@
         return packed + halves_sum(dot(here.astype(bf16), high_low(spread), 1, 0), width)
 
     def rows(self, values, at):
-        after_them = self.each - at - values.shape[1]
-        spaced = jnp.pad(values, ((0, 0), (at, after_them)), constant_values=-1)
-        return spaced.reshape(1, -1)
+        count = values.shape[1]
+        shape = (count, self.total)
+        row = (iota(shape, 1) & (self.each - 1)) - at
+        to = (row == iota(shape, 0)).astype(bf16)
+        high = values.astype(bf16)
+        low = (values - high.astype(f32)).astype(bf16)
+        spread = dot(high, to, 1, 0) + dot(low, to, 1, 0)
+        shape = (self.devices, self.total)
+        here = iota(shape, 1) >> log2(self.each) == iota(shape, 0)
+        flat = jnp.sum(jnp.where(here, spread, 0.0), axis=0, keepdims=True)
+        row = (iota((1, self.total), 1) & (self.each - 1)) - at
+        return jnp.where((row >= 0) & (row < count), flat.astype(jnp.int32), -1)
+
+    def biases(self, first, depth):
+        starts = (self.shared, self.shared + self.columns)
+        return [self.side_by_side(first, start, depth, 1, 0) for start in starts]
+
+    def side_by_side(self, values, first, depth, step, at):
+        shape = (values.shape[1], depth)
+        lane = (iota(shape, 1) & (self.columns - 1)) + first
+        spread = dot(values.astype(bf16), (lane == iota(shape, 0)).astype(bf16), 1, 0)
+        shape = (values.shape[0], depth)
+        here = iota(shape, 0) == (iota(shape, 1) >> log2(self.columns)) * step + at
+        return jnp.sum(jnp.where(here, spread, 0.0), axis=0, keepdims=True)
 
 
 def step_four(me, masks, parts, parts1, upstream, feat, biases, index, slots, bias1, packing, loose):
@@ -259,15 +288,16 @@
         first = w0[...].reshape(n * r, depth)
         second = w1[...].reshape(n * r, depth)
         total = jnp.zeros((1, depth), f32)
+        bias = packing.biases(biases_ref[...], depth)
         for at in chunks(samples):
             g = up[at].astype(f32)
             f = feat_ref[at]
             two = g * f
             total = total + jnp.sum(two, axis=0, keepdims=True)
             two_bf[at] = two.astype(bf16)
-            proj_one = dot(f.astype(bf16), first, 1, 1) + biases_ref[0:1]
+            proj_one = dot(f.astype(bf16), first, 1, 1) + bias[0]
             layer_bf[at] = (f * proj_one + f).astype(bf16)
-            proj_two = dot(layer_bf[at], second, 1, 1) + biases_ref[1:2]
+            proj_two = dot(layer_bf[at], second, 1, 1) + bias[1]
             layer = g + dot(two_bf[at], second, 1, 0)
             grad_feat = g * proj_two + layer * (proj_one + 1.0)
             grad_feat = grad_feat + dot((layer * f).astype(bf16), first, 1, 0)
@@ -300,21 +330,38 @@
     )
 
 
-def step_six(me, masks, parts, feat, bias):
-    n, r, depth = len(masks), parts[0].shape[1], feat.shape[1]
-    samples = feat.shape[0]
-
-    def body(me_ref, feat_ref, bias_ref, *refs):
-        part_refs, (out, wn) = refs[: len(parts)], refs[len(parts) :]
+def pick_next(index, values, packing):
+    width = values.shape[1]
+    rows = ((index >> log2(packing.shared)) << log2(packing.each)) + (
+        index & (packing.shared - 1)
+    )
+    both = high_low(values)
+    for k in range(index.shape[0]):
+        yield halves_sum(dot(one_hot(rows[k : k + 1], values.shape[0]), both, 0, 0), width)
+
+
+def step_six(me, masks, parts, index, back, packing):
+    n, r, depth = len(masks), parts[0].shape[1], parts[0].shape[2]
+    samples, width = index.shape[1], back.shape[1]
+
+    def body(me_ref, index_ref, back_ref, *refs):
+        part_refs, (out, wn, feat_ref) = refs[: len(parts)], refs[len(parts) :]
         put_parts(part_refs, wn, me_ref[0], masks)
         weights = wn[...].reshape(n * r, depth)
+        values = back_ref[...]
+        for k, picked in enumerate(pick_next(index_ref[...], values, packing)):
+            feat_ref[:, k * width : (k + 1) * width] = picked
+        bias = packing.side_by_side(values, 0, depth, packing.each, packing.bias_row)
         for at in chunks(samples):
             f = feat_ref[at]
-            proj = dot(f.astype(bf16), weights, 1, 1) + bias_ref[...]
+            proj = dot(f.astype(bf16), weights, 1, 1) + bias
             out[at] = (f * proj + f).astype(bf16)
 
     return call(
-        body, [((samples, depth), bf16)], [me, feat, bias, *parts], [((n, r, depth), bf16)]
+        body,
+        [((samples, depth), bf16)],
+        [me, index, back, *parts],
+        [((n, r, depth), bf16), ((samples, depth), f32)],
     )[0]
 
 
@@ -322,10 +369,10 @@
     return both[:, :width] + both[:, width:]
 
 
-def hot_update(me, rows, arrived, table, accum, bias, packing):
+def hot_update(me, first, arrived, table, accum, bias, packing):
     width = table.shape[1]
 
-    def body(me_ref, rows_ref, arrived_ref, table_ref, accum_ref, bias_ref, *outs):
+    def body(me_ref, first_ref, arrived_ref, table_ref, accum_ref, bias_ref, *outs):
         new, accum_new, returned, bias_new = outs
         values = arrived_ref[...]
         place = iota(values.shape, 0) & (packing.each - 1)
@@ -333,7 +380,9 @@
         bias_sum = jnp.sum(bias_sum, axis=0, keepdims=True)
         stepped = bias_ref[...] - bias_rate * bias_sum
         bias_new[...] = stepped
-        chosen = one_hot(rows_ref[...], table.shape[0])
+        rows = packing.rows(first_ref[:, : packing.shared], 0)
+        rows = jnp.where(rows < 0, -1, rows - me_ref[0] * table.shape[0])
+        chosen = one_hot(rows, table.shape[0])
         gradient = halves_sum(dot(chosen, high_low(values), 1, 0), width)
         updated, accum_new[...] = adagrad(table_ref[...], accum_ref[...], gradient, row_rate)
         new[...] = updated
@@ -345,40 +394,20 @@
     return call(
         body,
         [(table.shape, f32), (table.shape, f32), (arrived.shape, f32), ((1, width), f32)],
-        [me, rows, arrived, table, accum, bias],
-    )
-
-
-def pick_next(me, index, table, packing, depth):
-    fields, samples = index.shape
-    rows, width = table.shape
-
-    def body(me_ref, index_ref, table_ref, out, bias):
-        values = table_ref[...]
-        both = high_low(values)
-        for k in range(fields):
-            picked = dot(one_hot(index_ref[k : k + 1, :], rows), both, 0, 0)
-            out[:, k * width : (k + 1) * width] = halves_sum(picked, width)
-        shape = (width, depth)
-        lanes = (iota(shape, 1) & (packing.columns - 1)) == iota(shape, 0)
-        spread = dot(values.astype(bf16), lanes.astype(bf16), 1, 0)
-        shape = (rows, depth)
-        device = iota(shape, 1) >> log2(packing.columns)
-        here = iota(shape, 0) == (device << log2(packing.each)) + packing.bias_row
-        bias[...] = jnp.sum(jnp.where(here, spread, 0.0), axis=0, keepdims=True)
-
-    return call(body, [((samples, depth), f32), ((1, depth), f32)], [me, index, table])
-
-
-def owner_update(me, rows, moved, table, accum):
+        [me, first, arrived, table, accum, bias],
+    )
+
+
+def owner_update(me, targets, moved, table, accum, packing):
     width = table.shape[1]
 
-    def body(me_ref, rows_ref, moved_ref, table_ref, accum_ref, new, accum_new):
-        chosen = one_hot(rows_ref[...], table.shape[0])
+    def body(me_ref, targets_ref, moved_ref, table_ref, accum_ref, new, accum_new):
+        rows = packing.rows(targets_ref[...], packing.shared)
+        chosen = one_hot(rows, table.shape[0])
         gradient = halves_sum(dot(chosen, high_low(moved_ref[...]), 1, 0), width)
         new[...], accum_new[...] = adagrad(table_ref[...], accum_ref[...], gradient, row_rate)
 
-    return call(body, [(table.shape, f32), (table.shape, f32)], [me, rows, moved, table, accum])
+    return call(body, [(table.shape, f32), (table.shape, f32)], [me, targets, moved, table, accum])
 
 
 def plain_halves(grads, me, masks):
@@ -400,11 +429,12 @@
 def plain_four(me, masks, parts, parts1, upstream, feat, biases, index, slots, bias1, packing, loose):
     w0 = to_absolute(parts, me[0], len(masks))
     w1 = to_absolute(parts1, me[0], len(masks))
+    bias = packing.biases(biases, feat.shape[1])
     g = upstream.astype(f32)
     two = g * feat
-    proj_one = dot(feat.astype(bf16), w0, 1, 1) + biases[0:1]
+    proj_one = dot(feat.astype(bf16), w0, 1, 1) + bias[0]
     layer_bf = (feat * proj_one + feat).astype(bf16)
-    proj_two = dot(layer_bf, w1, 1, 1) + biases[1:2]
+    proj_two = dot(layer_bf, w1, 1, 1) + bias[1]
     layer = g + dot(two.astype(bf16), w1, 1, 0)
     one_bf = (layer * feat).astype(bf16)
     grad_feat = g * proj_two + layer * (proj_one + 1.0) + dot(one_bf, w0, 1, 0)
@@ -419,8 +449,10 @@
     return packed, keep, send
 
 
-def plain_six(me, masks, parts, feat, bias):
+def plain_six(me, masks, parts, index, back, packing):
     wn = to_absolute(parts, me[0], len(masks))
+    feat = jnp.concatenate(list(pick_next(index, back, packing)), axis=1)
+    bias = packing.side_by_side(back, 0, wn.shape[1], packing.each, packing.bias_row)
     proj = dot(feat.astype(bf16), wn, 1, 1) + bias
     return (feat * proj + feat).astype(bf16)
 
@@ -473,11 +505,11 @@
             w1_outer,
         ),
     )
-    arrived_ids = first[:, :per].astype(jnp.int32)
-    biases = first[:, per:].reshape(n, 2, columns).transpose(1, 0, 2).reshape(2, -1)
-
-    slot_values = jnp.concatenate([hot_cache, evict_cache], axis=0)
-    feat = pick(place, bag.T, slot_values)
+    packing = Packing(n, per, evict_dest.shape[2], columns)
+    bias_lanes = jnp.pad(cross_b.reshape(1, -1), ((0, 0), (0, width - 2 * columns)))
+    bias_lanes = pass_on(place, bias_lanes)
+
+    feat = pick(place, bag.T, hot_cache, evict_cache)
 
     def near_sum(keep, send):
         total, _ = sum_stage(keep, [send], groups[0], n)
@@ -492,7 +524,6 @@
     feat = after(feat, w0_outer)
     bias_one, keep0, send0 = two(place, masks, w1_parts, upstream, feat)
     keep0, parts0 = near_sum(keep0, send0)
-    packing = Packing(n, per, evict_dest.shape[2], columns)
     packed, keep1, send1 = four(
         place,
         masks,
@@ -500,7 +531,7 @@
         w1_parts,
         upstream,
         feat,
-        biases,
+        first,
         bag.T,
         slots,
         bias_one,
@@ -520,20 +551,16 @@
     w_new1, _ = adagrad(w_own[1], cross_accum.transpose(0, 2, 1)[1], grad1, weight_rate)
 
     arrived = exchange(packed.reshape(n, -1, width)).reshape(-1, width)
-    local_rows = packing.rows(arrived_ids - me * hot_table.shape[0], 0)
-    bias_lanes = jnp.pad(cross_b.reshape(1, -1), ((0, 0), (0, width - 2 * columns)))
     hot_new, hot_accum_new, returned, bias_new = hot_update(
-        place, local_rows, arrived, hot_table, hot_accum, bias_lanes, packing
+        place, first, arrived, hot_table, hot_accum, bias_lanes, packing
     )
     cross_b_new = bias_new[:, : 2 * columns].reshape(2, columns)
     back = exchange(returned.reshape(n, -1, width)).reshape(-1, width)
     owner_new, owner_accum_new = owner_update(
-        place, packing.rows(evict_dest[0], per), arrived, owner_table, owner_accum
-    )
-
-    next_rows = (next_bag // per) * packing.each + next_bag % per
-    next_feat, next_bias = pick_next(place, next_rows.T, back, packing, feat.shape[1])
-    next_first = six(place, masks, wn_parts, next_feat, next_bias)
+        place, evict_dest[0].astype(f32), arrived, owner_table, owner_accum, packing
+    )
+
+    next_first = six(place, masks, wn_parts, next_bag.T, back, packing)
     cross_w_new = jnp.stack([w_new0, w_new1]).transpose(0, 2, 1)
     return (
         next_first,

time: 156 us -> 164 us (1.051)
  waiting for transfers between devices: 38.8 us -> 55 us
  other arithmetic: 10.1 us -> 7 us
  local copies, waits for them, and re-layouts: 10.9 us -> 8.27 us
    all_to_all x2, waiting for transfers between devices: 0.01 us -> 8.68 us  [exchange(): lax.all_to_all(values, 'dev', split_axis=0, concat_axis=0, tiled=True)]
    ppermute x44, waiting for transfers between devices: 38.8 us -> 46.4 us  [swap(): return lax.ppermute(values, 'dev', [(i, i ^ mask) for i in range(devices)])]
    reshape x5 -> x0, local copies, waits for them, and re-layouts: 2.12 us -> none  [the longest x2 1.34 us: rows(): return spaced.reshape(1, -1)]
    another operation x4, other arithmetic: 5.64 us -> 3.8 us
    unnamed x55 -> x54, local copies, waits for them, and re-layouts: 5.09 us -> 4.24 us
  transfers between devices with their start and end apart: 46 -> 46, of which waited for: 16 -> 14; matrix products, arithmetic and copies ran while one was open for 9% -> 6% of each run, Pallas kernels for 18% -> 16%
where the time goes in v1:
time: 164 us
  waiting for transfers between devices  55 us (34%)
  starting transfers between devices  48.5 us (30%)
  Pallas kernels  32.8 us (20%)
  blocking collectives  10.9 us (7%)
  local copies, waits for them, and re-layouts  8.27 us (5%)
  other arithmetic  7 us (4%)
    ppermute x44, waiting for transfers between devices, swap(): return lax.ppermute(values, 'dev', [(i, i ^ mask) for i in range(devices)])  46.4 us
    ppermute x44, starting transfers between devices, swap(): return lax.ppermute(values, 'dev', [(i, i ^ mask) for i in range(devices)])  40.5 us
    pallas_call x7, Pallas kernels, call(): pl.pallas_call(kernel, out_shape=[jax.ShapeDtypeStruct(*out) for out in o...  32.8 us
    all_to_all x1, blocking collectives, exchange(): lax.all_to_all(values, 'dev', split_axis=0, concat_axis=0, tiled=True)  10.9 us
    all_to_all x2, waiting for transfers between devices, exchange(): lax.all_to_all(values, 'dev', split_axis=0, concat_axis=0, tiled=True)  8.68 us
    all_to_all x2, starting transfers between devices, exchange(): lax.all_to_all(values, 'dev', split_axis=0, concat_axis=0, tiled=True)  8.02 us
    unnamed x54, local copies, waits for them, and re-layouts  4.24 us
    another operation x4, other arithmetic  3.8 us
  transfers between devices with their start and end apart: 46, of which 14 were waited for; matrix products, arithmetic and copies ran while one was open for 6% of the time, Pallas kernels for 16%

profile of v1, /device:TPU:0, one launch (start us, length us, event | category | flops | bytes accessed | tf_op | source)
XLA Modules:
  0.0 163.6 jit_solution(2764715131189555616)
XLA Ops:
  0.6 1.0 fusion.14
  1.6 3.1 %collective-permute-start = (bf16[1,32,1024]{2,1,0:T(8,128)(2,1)S(1)}, bf16[1,32,1024]{2,1,0:T(8,128)(2,1)S(1)}, u32[]{:S(2)}, u32[]{:S(2)}) collective-permute-start(bf16[1,32,1024]{2,1,0:T(8,128)(2,1)S(1)} %get-tuple-element.68), channel_id=1, source_target_pairs={{0,8},{1,9},{2,10},{3,11},{4,12},{5,13},{6,14},{7,15},{8,0},{9,1},... | collective-permute-start | bytes 196616 | tf_op jit(solution)/shard_map/ppermute | solution.py:44
  4.7 2.6 %collective-permute-start.1 = (bf16[1,32,1024]{2,1,0:T(8,128)(2,1)S(1)}, bf16[1,32,1024]{2,1,0:T(8,128)(2,1)S(1)}, u32[]{:S(2)}, u32[]{:S(2)}) collective-permute-start(bf16[1,32,1024]{2,1,0:T(8,128)(2,1)S(1)} %get-tuple-element.68), channel_id=1, source_target_pairs={{0,16},{1,17},{2,18},{3,19},{4,20},{5,21},{6,22},{7,23},{8,24},{9,... | collective-permute-start | bytes 196616 | tf_op jit(solution)/shard_map/ppermute | solution.py:44
  7.3 4.7 %collective-permute-done.1 = bf16[1,32,1024]{2,1,0:T(8,128)(2,1)S(1)} collective-permute-done((bf16[1,32,1024]{2,1,0:T(8,128)(2,1)S(1)}, bf16[1,32,1024]{2,1,0:T(8,128)(2,1)S(1)}, u32[]{:S(2)}, u32[]{:S(2)}) %collective-permute-start.1) | collective-permute-done | bytes 65568 | tf_op jit(solution)/shard_map/ppermute | solution.py:44
  12.0 1.4 collective-permute-done.2
  13.5 1.6 collective-permute-start.6
  15.0 1.5 collective-permute-start.7
  17.0 5.7 %collective-permute-done.6.refs_4_.refs_15_ = bf16[4,32,1024]{2,1,0:T(8,128)(2,1)S(1)} collective-permute-done((bf16[4,32,1024]{2,1,0:T(8,128)(2,1)S(1)}, bf16[4,32,1024]{2,1,0:T(8,128)(2,1)S(1)}, u32[]{:S(2)}, u32[]{:S(2)}) %collective-permute-start.6) | collective-permute-done | bytes 262176 | tf_op jit(solution)/shard_map/ppermute | solution.py:44
  22.7 4.1 %collective-permute-done.7.refs_5_.refs_16_ = bf16[4,32,1024]{2,1,0:T(8,128)(2,1)S(1)} collective-permute-done((bf16[4,32,1024]{2,1,0:T(8,128)(2,1)S(1)}, bf16[4,32,1024]{2,1,0:T(8,128)(2,1)S(1)}, u32[]{:S(2)}, u32[]{:S(2)}) %collective-permute-start.7) | collective-permute-done | bytes 262176 | tf_op jit(solution)/shard_map/ppermute | solution.py:44
  27.3 2.1 %collective-permute-start.4 = (bf16[1,32,1024]{2,1,0:T(8,128)(2,1)S(1)}, bf16[1,32,1024]{2,1,0:T(8,128)(2,1)S(1)}, u32[]{:S(2)}, u32[]{:S(2)}) collective-permute-start(bf16[1,32,1024]{2,1,0:T(8,128)(2,1)S(1)} %bitcast.27), channel_id=1, source_target_pairs={{0,16},{1,17},{2,18},{3,19},{4,20},{5,21},{6,22},{7,23},{8,24},{9,... | collective-permute-start | bytes 196616 | tf_op jit(solution)/shard_map/ppermute | solution.py:44
  29.4 4.3 %collective-permute-done.4 = bf16[1,32,1024]{2,1,0:T(8,128)(2,1)S(1)} collective-permute-done((bf16[1,32,1024]{2,1,0:T(8,128)(2,1)S(1)}, bf16[1,32,1024]{2,1,0:T(8,128)(2,1)S(1)}, u32[]{:S(2)}, u32[]{:S(2)}) %collective-permute-start.4) | collective-permute-done | bytes 65568 | tf_op jit(solution)/shard_map/ppermute | solution.py:44
  33.7 2.9 %shard_map.189.refs_2_ = f32[512,1024]{1,0:T(8,128)} custom-call(s32[1]{0:T(128)} %bitcast.refs_0_, s32[8,512]{1,0:T(8,128)} %bitcast.33, f32[128,128]{1,0:T(8,128)} %refs_2_.1, f32[64,128]{1,0:T(8,128)} %refs_3_.3), custom_call_target="tpu_custom_call" | custom-call | tf_op jit(solution)/shard_map/pallas_call | solution.py:115
  36.6 3.1 %collective-permute-done.5 = bf16[1,32,1024]{2,1,0:T(8,128)(2,1)S(1)} collective-permute-done((bf16[1,32,1024]{2,1,0:T(8,128)(2,1)S(1)}, bf16[1,32,1024]{2,1,0:T(8,128)(2,1)S(1)}, u32[]{:S(2)}, u32[]{:S(2)}) %collective-permute-start.5) | collective-permute-done | bytes 65568 | tf_op jit(solution)/shard_map/ppermute | solution.py:44
  39.9 0.6 copy-done.11
  40.7 0.7 copy-done.14
  41.4 6.8 %shard_map.190 = (f32[1,1024]{1,0:T(1,128)}, f32[16,32,1024]{2,1,0:T(8,128)}, bf16[16,32,1024]{2,1,0:T(8,128)(2,1)}) custom-call(s32[1]{0:T(128)} %bitcast.refs_0_, bf16[512,1024]{1,0:T(8,128)(2,1)} %refs_1_.3, f32[512,1024]{1,0:T(8,128)} %shard_map.189.refs_2_, bf16[4,32,1024]{2,1,0:T(8,128)(2,1)} %copy-done, bf16[4,32,1024]{2,1,0:T(8,128)(2,1)} %copy-done.8, ...), custom_call_target="tpu_custom_call" | custom-call | tf_op jit(solution)/shard_map/pallas_call | solution.py:115
  48.2 1.1 collective-permute-start.13
  49.3 0.9 collective-permute-start.14
  50.2 1.4 collective-permute-start.15
  52.0 5.5 %collective-permute-done.13.refs_7_ = bf16[4,32,1024]{2,1,0:T(8,128)(2,1)} collective-permute-done((bf16[4,32,1024]{2,1,0:T(8,128)(2,1)S(1)}, bf16[4,32,1024]{2,1,0:T(8,128)(2,1)}, u32[]{:S(2)}, u32[]{:S(2)}) %collective-permute-start.13) | collective-permute-done | bytes 262176 | tf_op jit(solution)/shard_map/ppermute | solution.py:44
  57.5 4.4 %collective-permute-done.14.refs_8_ = bf16[4,32,1024]{2,1,0:T(8,128)(2,1)} collective-permute-done((bf16[4,32,1024]{2,1,0:T(8,128)(2,1)S(1)}, bf16[4,32,1024]{2,1,0:T(8,128)(2,1)}, u32[]{:S(2)}, u32[]{:S(2)}) %collective-permute-start.14) | collective-permute-done | bytes 262176 | tf_op jit(solution)/shard_map/ppermute | solution.py:44
  61.8 1.7 %collective-permute-done.15.refs_9_ = bf16[4,32,1024]{2,1,0:T(8,128)(2,1)} collective-permute-done((bf16[4,32,1024]{2,1,0:T(8,128)(2,1)S(1)}, bf16[4,32,1024]{2,1,0:T(8,128)(2,1)}, u32[]{:S(2)}, u32[]{:S(2)}) %collective-permute-start.15) | collective-permute-done | bytes 262176 | tf_op jit(solution)/shard_map/ppermute | solution.py:44
  63.6 2.0 %fusion.20 = (bf16[16,32,1024]{2,1,0:T(8,128)(2,1)S(1)}, f32[16,32,1024]{2,1,0:T(8,128)S(1)}) fusion(f32[16,32,1024]{2,1,0:T(8,128)} %get-tuple-element.32, bf16[16,32,1024]{2,1,0:T(8,128)(2,1)S(1)} %collective-permute-done.20), kind=kLoop, calls=%fused_computation.35 | loop fusion | flops 1572864 | bytes 6291456 | tf_op jit(solution)/shard_map/convert.12
  65.7 1.4 collective-permute-start.21
  67.1 1.5 collective-permute-start.22
  68.6 0.7 copy-done.21
  69.3 0.7 collective-permute-start.23
  70.0 10.9 %all_to_all.21 = f32[32,1,68]{2,1,0:T(1,128)} all-to-all(f32[32,1,68]{2,1,0:T(1,128)S(1)} %bitcast.35), channel_id=1, replica_groups=mesh['dev'=32] {'dev'}, dimensions={0} | all-to-all | bytes 17408 | tf_op jit(solution)/shard_map/all_to_all | solution.py:95
  80.9 12.3 %shard_map.191 = (f32[256,128]{1,0:T(8,128)}, f32[16,32,1024]{2,1,0:T(8,128)}, bf16[16,32,1024]{2,1,0:T(8,128)(2,1)}) custom-call(s32[1]{0:T(128)} %bitcast.refs_0_, bf16[512,1024]{1,0:T(8,128)(2,1)} %refs_1_.3, f32[512,1024]{1,0:T(8,128)} %shard_map.189.refs_2_, f32[32,68]{1,0:T(8,128)} %bitcast.30, s32[8,512]{1,0:T(8,128)} %bitcast.34, ...), custom_call_target="tpu_custom_call" | custom-call | tf_op jit(solution)/shard_map/pallas_call | solution.py:115
  93.4 1.3 fusion.18
  94.8 1.2 collective-permute-start.25
  96.0 3.1 %collective-permute-start.26 = (bf16[1,32,1024]{2,1,0:T(8,128)(2,1)S(1)}, bf16[1,32,1024]{2,1,0:T(8,128)(2,1)S(1)}, u32[]{:S(2)}, u32[]{:S(2)}) collective-permute-start(bf16[1,32,1024]{2,1,0:T(8,128)(2,1)S(1)} %get-tuple-element.65), channel_id=1, source_target_pairs={{0,24},{1,25},{2,26},{3,27},{4,28},{5,29},{6,30},{7,31},{8,16},{9,... | collective-permute-start | bytes 196616 | tf_op jit(solution)/shard_map/ppermute | solution.py:44
  99.2 1.1 collective-permute-done.24
  100.3 3.2 %collective-permute-done.25 = bf16[1,32,1024]{2,1,0:T(8,128)(2,1)S(1)} collective-permute-done((bf16[1,32,1024]{2,1,0:T(8,128)(2,1)S(1)}, bf16[1,32,1024]{2,1,0:T(8,128)(2,1)S(1)}, u32[]{:S(2)}, u32[]{:S(2)}) %collective-permute-start.25) | collective-permute-done | bytes 65568 | tf_op jit(solution)/shard_map/ppermute | solution.py:44
  103.5 1.0 fusion.16
  104.5 1.5 collective-permute-start.27
  106.1 0.8 collective-permute-start.28
  106.9 2.1 %collective-permute-start.29 = (bf16[1,32,1024]{2,1,0:T(8,128)(2,1)S(1)}, bf16[1,32,1024]{2,1,0:T(8,128)(2,1)S(1)}, u32[]{:S(2)}, u32[]{:S(2)}) collective-permute-start(bf16[1,32,1024]{2,1,0:T(8,128)(2,1)S(1)} %get-tuple-element.49), channel_id=1, source_target_pairs={{0,24},{1,25},{2,26},{3,27},{4,28},{5,29},{6,30},{7,31},{8,16},{9,... | collective-permute-start | bytes 196616 | tf_op jit(solution)/shard_map/ppermute | solution.py:44
  109.0 4.6 %collective-permute-done.28 = bf16[1,32,1024]{2,1,0:T(8,128)(2,1)S(1)} collective-permute-done((bf16[1,32,1024]{2,1,0:T(8,128)(2,1)S(1)}, bf16[1,32,1024]{2,1,0:T(8,128)(2,1)S(1)}, u32[]{:S(2)}, u32[]{:S(2)}) %collective-permute-start.28) | collective-permute-done | bytes 65568 | tf_op jit(solution)/shard_map/ppermute | solution.py:44
  113.7 1.4 collective-permute-start.30
  115.1 0.7 collective-permute-start.31
  115.8 1.4 collective-permute-start.32
  117.7 0.8 fusion.21
  118.5 1.3 collective-permute-start.38
  119.8 0.7 collective-permute-start.39
  120.5 2.4 %collective-permute-done.30.refs_4_ = bf16[4,32,1024]{2,1,0:T(8,128)(2,1)S(1)} collective-permute-done((bf16[4,32,1024]{2,1,0:T(8,128)(2,1)S(1)}, bf16[4,32,1024]{2,1,0:T(8,128)(2,1)S(1)}, u32[]{:S(2)}, u32[]{:S(2)}) %collective-permute-start.30) | collective-permute-done | bytes 262176 | tf_op jit(solution)/shard_map/ppermute | solution.py:44
  122.9 1.5 collective-permute-start.40
  124.4 3.1 %all-to-all-start.1 = ((f32[32,8,128]{2,1,0:T(8,128)}), f32[32,8,128]{2,1,0:T(8,128)S(1)}, u32[]{:S(2)}, u32[]{:S(2)}) async-start(f32[32,8,128]{2,1,0:T(8,128)} %bitcast.8), calls=%async_computation.1 | async-start | bytes 262144 | tf_op jit(solution)/shard_map/all_to_all | solution.py:95
  127.6 0.5 pad.4.refs_1_
  128.1 1.2 shard_map.192.refs_5_
  129.3 0.7 copy.23.refs_1_
  130.0 8.7 %all-to-all-done.1 = f32[32,8,128]{2,1,0:T(8,128)S(1)} async-done(((f32[32,8,128]{2,1,0:T(8,128)}), f32[32,8,128]{2,1,0:T(8,128)S(1)}, u32[]{:S(2)}, u32[]{:S(2)}) %all-to-all-start.1) | async-done | bytes 131104 | tf_op jit(solution)/shard_map/all_to_all | solution.py:95
  138.6 0.7 copy-done.2
  139.3 2.0 %shard_map.193 = (f32[64,128]{1,0:T(8,128)}, f32[64,128]{1,0:T(8,128)}, f32[256,128]{1,0:T(8,128)}, f32[1,128]{1,0:T(1,128)}) custom-call(s32[1]{0:T(128)} %bitcast.refs_0_, f32[32,68]{1,0:T(8,128)} %bitcast.31, f32[256,128]{1,0:T(8,128)} %bitcast.18, f32[64,128]{1,0:T(8,128)} %refs_3_.4, f32[64,128]{1,0:T(8,128)} %refs_4_.2, f32[1,128]{1,0:T(1,128)} %shard_map.192.refs_5_), custom_call_target="tpu_custom_call" | custom-call | tf_op jit(solution)/shard_map/pallas_call | solution.py:115
  141.3 5.0 %all-to-all-start.2 = ((f32[32,8,128]{2,1,0:T(8,128)}), f32[32,8,128]{2,1,0:T(8,128)S(1)}, u32[]{:S(2)}, u32[]{:S(2)}) async-start(f32[32,8,128]{2,1,0:T(8,128)} %bitcast.32), calls=%async_computation.2 | async-start | bytes 262144 | tf_op jit(solution)/shard_map/all_to_all | solution.py:95
  147.4 1.2 fusion.1
  148.7 1.6 collective-permute-start.41
  150.3 0.7 copy-done.19
  151.1 2.4 %collective-permute-start.42 = (bf16[1,32,1024]{2,1,0:T(8,128)(2,1)S(1)}, bf16[1,32,1024]{2,1,0:T(8,128)(2,1)S(1)}, u32[]{:S(2)}, u32[]{:S(2)}) collective-permute-start(bf16[1,32,1024]{2,1,0:T(8,128)(2,1)S(1)} %get-tuple-element.63), channel_id=1, source_target_pairs={{0,16},{1,17},{2,18},{3,19},{4,20},{5,21},{6,22},{7,23},{8,24},{9,... | collective-permute-start | bytes 196616 | tf_op jit(solution)/shard_map/ppermute | solution.py:44
  153.9 0.6 reshape.97
  154.6 2.8 %shard_map.195 = (f32[1024,128]{1,0:T(8,128)}, f32[1024,128]{1,0:T(8,128)}) custom-call(s32[1]{0:T(128)} %bitcast.refs_0_, f32[32,2]{1,0:T(8,128)} %copy.23.refs_1_, f32[256,128]{1,0:T(8,128)} %bitcast.19, f32[1024,128]{1,0:T(8,128)} %refs_3_.5, f32[1024,128]{1,0:T(8,128)} %refs_4_.3), custom_call_target="tpu_custom_call" | custom-call | tf_op jit(solution)/shard_map/pallas_call | solution.py:115
  157.4 0.6 copy-done.16
  158.0 4.7 %shard_map.194 = bf16[512,1024]{1,0:T(8,128)(2,1)} custom-call(s32[1]{0:T(128)} %bitcast.refs_0_, s32[8,512]{1,0:T(8,128)} %bitcast.36, f32[256,128]{1,0:T(8,128)} %bitcast.23, bf16[4,32,1024]{2,1,0:T(8,128)(2,1)} %copy-done.3, bf16[4,32,1024]{2,1,0:T(8,128)(2,1)} %copy-done.18, bf16[4,32,1024]{2,1,0:T(8,128)(2,1)} %collective-permute-done.31.refs_5_, ...), custom_call_target="tpu_custom_call" | custom-call | tf_op jit(solution)/shard_map/pallas_call | solution.py:115
  162.9 0.7 maximum_bitcast_fusion
  (118 shorter events, 4.2 us)
Async XLA Ops:
  1.6 5.7 %collective-permute-start = (bf16[1,32,1024]{2,1,0:T(8,128)(2,1)S(1)}, bf16[1,32,1024]{2,1,0:T(8,128)(2,1)S(1)}, u32[]{:S(2)}, u32[]{:S(2)}) collective-permute-start(bf16[1,32,1024]{2,1,0:T(8,128)(2,1)S(1)} %get-tuple-element.68), channel_id=1, source_target_pairs={{0,8},{1,9},{2,10},{3,11},{4,12},{5,13},{6,14},{7,15},{8,0},{9,1},... | collective-permute-start | bytes 196616 | tf_op jit(solution)/shard_map/ppermute | solution.py:44
  4.7 7.3 %collective-permute-start.1 = (bf16[1,32,1024]{2,1,0:T(8,128)(2,1)S(1)}, bf16[1,32,1024]{2,1,0:T(8,128)(2,1)S(1)}, u32[]{:S(2)}, u32[]{:S(2)}) collective-permute-start(bf16[1,32,1024]{2,1,0:T(8,128)(2,1)S(1)} %get-tuple-element.68), channel_id=1, source_target_pairs={{0,16},{1,17},{2,18},{3,19},{4,20},{5,21},{6,22},{7,23},{8,24},{9,... | collective-permute-start | bytes 196616 | tf_op jit(solution)/shard_map/ppermute | solution.py:44
  7.3 6.1 %collective-permute-start.2 = (bf16[1,32,1024]{2,1,0:T(8,128)(2,1)S(1)}, bf16[1,32,1024]{2,1,0:T(8,128)(2,1)S(1)}, u32[]{:S(2)}, u32[]{:S(2)}) collective-permute-start(bf16[1,32,1024]{2,1,0:T(8,128)(2,1)S(1)} %get-tuple-element.68), channel_id=1, source_target_pairs={{0,24},{1,25},{2,26},{3,27},{4,28},{5,29},{6,30},{7,31},{8,16},{9,... | collective-permute-start | bytes 196616 | tf_op jit(solution)/shard_map/ppermute | solution.py:44
  13.4 26.5 %copy-start = (bf16[4,32,1024]{2,1,0:T(8,128)(2,1)}, bf16[4,32,1024]{2,1,0:T(8,128)(2,1)S(1)}, u32[]{:S(2)}) copy-start(bf16[4,32,1024]{2,1,0:T(8,128)(2,1)S(1)} %pad_maximum_fusion.refs_3_.refs_14_) | copy-start | bytes 786436
  13.5 9.2 %collective-permute-start.6 = (bf16[4,32,1024]{2,1,0:T(8,128)(2,1)S(1)}, bf16[4,32,1024]{2,1,0:T(8,128)(2,1)S(1)}, u32[]{:S(2)}, u32[]{:S(2)}) collective-permute-start(bf16[4,32,1024]{2,1,0:T(8,128)(2,1)S(1)} %pad_maximum_fusion.refs_3_.refs_14_), channel_id=1, source_target_pairs={{0,2},{1,3},{2,0},{3,1},{4,6},{5,7},{6,4},{7,5},{8,10},{9,11},{10,... | collective-permute-start | bytes 786440 | tf_op jit(solution)/shard_map/ppermute | solution.py:44
  15.0 11.8 %collective-permute-start.7 = (bf16[4,32,1024]{2,1,0:T(8,128)(2,1)S(1)}, bf16[4,32,1024]{2,1,0:T(8,128)(2,1)S(1)}, u32[]{:S(2)}, u32[]{:S(2)}) collective-permute-start(bf16[4,32,1024]{2,1,0:T(8,128)(2,1)S(1)} %pad_maximum_fusion.refs_3_.refs_14_), channel_id=1, source_target_pairs={{0,4},{1,5},{2,6},{3,7},{4,0},{5,1},{6,2},{7,3},{8,12},{9,13},{10,... | collective-permute-start | bytes 786440 | tf_op jit(solution)/shard_map/ppermute | solution.py:44
  16.5 10.3 %collective-permute-start.8 = (bf16[4,32,1024]{2,1,0:T(8,128)(2,1)S(1)}, bf16[4,32,1024]{2,1,0:T(8,128)(2,1)S(1)}, u32[]{:S(2)}, u32[]{:S(2)}) collective-permute-start(bf16[4,32,1024]{2,1,0:T(8,128)(2,1)S(1)} %pad_maximum_fusion.refs_3_.refs_14_), channel_id=1, source_target_pairs={{0,6},{1,7},{2,4},{3,5},{4,2},{5,3},{6,0},{7,1},{8,14},{9,15},{10,... | collective-permute-start | bytes 786440 | tf_op jit(solution)/shard_map/ppermute | solution.py:44
  17.0 10.3 %collective-permute-start.3 = (bf16[1,32,1024]{2,1,0:T(8,128)(2,1)S(1)}, bf16[1,32,1024]{2,1,0:T(8,128)(2,1)S(1)}, u32[]{:S(2)}, u32[]{:S(2)}) collective-permute-start(bf16[1,32,1024]{2,1,0:T(8,128)(2,1)S(1)} %bitcast.26), channel_id=1, source_target_pairs={{0,8},{1,9},{2,10},{3,11},{4,12},{5,13},{6,14},{7,15},{8,0},{9,1},... | collective-permute-start | bytes 196616 | tf_op jit(solution)/shard_map/ppermute | solution.py:44
  17.0 22.8 %collective-permute-start.9 = (bf16[4,32,1024]{2,1,0:T(8,128)(2,1)S(1)}, bf16[4,32,1024]{2,1,0:T(8,128)(2,1)S(1)}, u32[]{:S(2)}, u32[]{:S(2)}) collective-permute-start(bf16[4,32,1024]{2,1,0:T(8,128)(2,1)S(1)} %pad_maximum_fusion.refs_3_.refs_14_), channel_id=1, source_target_pairs={{0,1},{1,0},{2,3},{3,2},{4,5},{5,4},{6,7},{7,6},{8,9},{9,8},{10,11... | collective-permute-start | bytes 786440 | tf_op jit(solution)/shard_map/ppermute | solution.py:44
  22.7 17.2 %copy-start.8 = (bf16[4,32,1024]{2,1,0:T(8,128)(2,1)}, bf16[4,32,1024]{2,1,0:T(8,128)(2,1)S(1)}, u32[]{:S(2)}) copy-start(bf16[4,32,1024]{2,1,0:T(8,128)(2,1)S(1)} %collective-permute-done.6.refs_4_.refs_15_) | copy-start | bytes 786436
  22.7 17.1 %collective-permute-start.10 = (bf16[4,32,1024]{2,1,0:T(8,128)(2,1)S(1)}, bf16[4,32,1024]{2,1,0:T(8,128)(2,1)S(1)}, u32[]{:S(2)}, u32[]{:S(2)}) collective-permute-start(bf16[4,32,1024]{2,1,0:T(8,128)(2,1)S(1)} %collective-permute-done.6.refs_4_.refs_15_), channel_id=1, source_target_pairs={{0,1},{1,0},{2,3},{3,2},{4,5},{5,4},{6,7},{7,6},{8,9},{9,8},{10,11... | collective-permute-start | bytes 786440 | tf_op jit(solution)/shard_map/ppermute | solution.py:44
  26.8 13.1 %copy-start.9 = (bf16[4,32,1024]{2,1,0:T(8,128)(2,1)}, bf16[4,32,1024]{2,1,0:T(8,128)(2,1)S(1)}, u32[]{:S(2)}) copy-start(bf16[4,32,1024]{2,1,0:T(8,128)(2,1)S(1)} %collective-permute-done.7.refs_5_.refs_16_) | copy-start | bytes 786436
  26.8 13.1 %collective-permute-start.11 = (bf16[4,32,1024]{2,1,0:T(8,128)(2,1)S(1)}, bf16[4,32,1024]{2,1,0:T(8,128)(2,1)S(1)}, u32[]{:S(2)}, u32[]{:S(2)}) collective-permute-start(bf16[4,32,1024]{2,1,0:T(8,128)(2,1)S(1)} %collective-permute-done.7.refs_5_.refs_16_), channel_id=1, source_target_pairs={{0,1},{1,0},{2,3},{3,2},{4,5},{5,4},{6,7},{7,6},{8,9},{9,8},{10,11... | collective-permute-start | bytes 786440 | tf_op jit(solution)/shard_map/ppermute | solution.py:44
  26.8 13.1 %copy-start.10 = (bf16[4,32,1024]{2,1,0:T(8,128)(2,1)}, bf16[4,32,1024]{2,1,0:T(8,128)(2,1)S(1)}, u32[]{:S(2)}) copy-start(bf16[4,32,1024]{2,1,0:T(8,128)(2,1)S(1)} %collective-permute-done.8.refs_6_.refs_17_) | copy-start | bytes 786436
  26.8 13.1 %collective-permute-start.12 = (bf16[4,32,1024]{2,1,0:T(8,128)(2,1)S(1)}, bf16[4,32,1024]{2,1,0:T(8,128)(2,1)S(1)}, u32[]{:S(2)}, u32[]{:S(2)}) collective-permute-start(bf16[4,32,1024]{2,1,0:T(8,128)(2,1)S(1)} %collective-permute-done.8.refs_6_.refs_17_), channel_id=1, source_target_pairs={{0,1},{1,0},{2,3},{3,2},{4,5},{5,4},{6,7},{7,6},{8,9},{9,8},{10,11... | collective-permute-start | bytes 786440 | tf_op jit(solution)/shard_map/ppermute | solution.py:44
  27.3 6.4 %collective-permute-start.4 = (bf16[1,32,1024]{2,1,0:T(8,128)(2,1)S(1)}, bf16[1,32,1024]{2,1,0:T(8,128)(2,1)S(1)}, u32[]{:S(2)}, u32[]{:S(2)}) collective-permute-start(bf16[1,32,1024]{2,1,0:T(8,128)(2,1)S(1)} %bitcast.27), channel_id=1, source_target_pairs={{0,16},{1,17},{2,18},{3,19},{4,20},{5,21},{6,22},{7,23},{8,24},{9,... | collective-permute-start | bytes 196616 | tf_op jit(solution)/shard_map/ppermute | solution.py:44
  33.7 6.1 %collective-permute-start.5 = (bf16[1,32,1024]{2,1,0:T(8,128)(2,1)S(1)}, bf16[1,32,1024]{2,1,0:T(8,128)(2,1)S(1)}, u32[]{:S(2)}, u32[]{:S(2)}) collective-permute-start(bf16[1,32,1024]{2,1,0:T(8,128)(2,1)S(1)} %bitcast.28), channel_id=1, source_target_pairs={{0,24},{1,25},{2,26},{3,27},{4,28},{5,29},{6,30},{7,31},{8,16},{9,... | collective-permute-start | bytes 196616 | tf_op jit(solution)/shard_map/ppermute | solution.py:44
  39.8 12.2 %copy-start.4 = (bf16[4,32,1024]{2,1,0:T(8,128)(2,1)}, bf16[4,32,1024]{2,1,0:T(8,128)(2,1)S(1)}, u32[]{:S(2)}) copy-start(bf16[4,32,1024]{2,1,0:T(8,128)(2,1)S(1)} %pad_maximum_fusion.1.refs_6_) | copy-start | bytes 786436
  39.8 11.9 %copy-start.25 = (s32[128]{0:T(128)S(1)}, s32[128]{0:T(128)}, u32[]{:S(2)}) copy-start(s32[128]{0:T(128)} %param.17) | copy-start | bytes 1540
  39.8 12.0 %copy-start.22 = (f32[2,32]{1,0:T(2,128)S(1)}, f32[2,32]{1,0:T(2,128)}, u32[]{:S(2)}) copy-start(f32[2,32]{1,0:T(2,128)} %param.26) | copy-start | bytes 772
  48.2 15.4 %collective-permute-start.20 = (bf16[16,32,1024]{2,1,0:T(8,128)(2,1)}, bf16[16,32,1024]{2,1,0:T(8,128)(2,1)S(1)}, u32[]{:S(2)}, u32[]{:S(2)}) collective-permute-start(bf16[16,32,1024]{2,1,0:T(8,128)(2,1)} %get-tuple-element.33), channel_id=1, source_target_pairs={{0,1},{1,0},{2,3},{3,2},{4,5},{5,4},{6,7},{7,6},{8,9},{9,8},{10,11... | collective-permute-start | bytes 3145736 | tf_op jit(solution)/shard_map/ppermute | solution.py:44
  48.2 9.3 %collective-permute-start.13 = (bf16[4,32,1024]{2,1,0:T(8,128)(2,1)S(1)}, bf16[4,32,1024]{2,1,0:T(8,128)(2,1)}, u32[]{:S(2)}, u32[]{:S(2)}) collective-permute-start(bf16[4,32,1024]{2,1,0:T(8,128)(2,1)S(1)} %pad_maximum_fusion.1.refs_6_), channel_id=1, source_target_pairs={{0,2},{1,3},{2,0},{3,1},{4,6},{5,7},{6,4},{7,5},{8,10},{9,11},{10,... | collective-permute-start | bytes 786440 | tf_op jit(solution)/shard_map/ppermute | solution.py:44
  49.3 12.5 %collective-permute-start.14 = (bf16[4,32,1024]{2,1,0:T(8,128)(2,1)S(1)}, bf16[4,32,1024]{2,1,0:T(8,128)(2,1)}, u32[]{:S(2)}, u32[]{:S(2)}) collective-permute-start(bf16[4,32,1024]{2,1,0:T(8,128)(2,1)S(1)} %pad_maximum_fusion.1.refs_6_), channel_id=1, source_target_pairs={{0,4},{1,5},{2,6},{3,7},{4,0},{5,1},{6,2},{7,3},{8,12},{9,13},{10,... | collective-permute-start | bytes 786440 | tf_op jit(solution)/shard_map/ppermute | solution.py:44
  50.2 13.3 %collective-permute-start.15 = (bf16[4,32,1024]{2,1,0:T(8,128)(2,1)S(1)}, bf16[4,32,1024]{2,1,0:T(8,128)(2,1)}, u32[]{:S(2)}, u32[]{:S(2)}) collective-permute-start(bf16[4,32,1024]{2,1,0:T(8,128)(2,1)S(1)} %pad_maximum_fusion.1.refs_6_), channel_id=1, source_target_pairs={{0,6},{1,7},{2,4},{3,5},{4,2},{5,3},{6,0},{7,1},{8,14},{9,15},{10,... | collective-permute-start | bytes 786440 | tf_op jit(solution)/shard_map/ppermute | solution.py:44
  52.0 15.1 %collective-permute-start.16 = (bf16[4,32,1024]{2,1,0:T(8,128)(2,1)S(1)}, bf16[4,32,1024]{2,1,0:T(8,128)(2,1)S(1)}, u32[]{:S(2)}, u32[]{:S(2)}) collective-permute-start(bf16[4,32,1024]{2,1,0:T(8,128)(2,1)S(1)} %pad_maximum_fusion.1.refs_6_), channel_id=1, source_target_pairs={{0,1},{1,0},{2,3},{3,2},{4,5},{5,4},{6,7},{7,6},{8,9},{9,8},{10,11... | collective-permute-start | bytes 786440 | tf_op jit(solution)/shard_map/ppermute | solution.py:44
  57.5 11.1 %collective-permute-start.17 = (bf16[4,32,1024]{2,1,0:T(8,128)(2,1)}, bf16[4,32,1024]{2,1,0:T(8,128)(2,1)S(1)}, u32[]{:S(2)}, u32[]{:S(2)}) collective-permute-start(bf16[4,32,1024]{2,1,0:T(8,128)(2,1)} %collective-permute-done.13.refs_7_), channel_id=1, source_target_pairs={{0,1},{1,0},{2,3},{3,2},{4,5},{5,4},{6,7},{7,6},{8,9},{9,8},{10,11... | collective-permute-start | bytes 786440 | tf_op jit(solution)/shard_map/ppermute | solution.py:44
  61.8 19.0 %collective-permute-start.18 = (bf16[4,32,1024]{2,1,0:T(8,128)(2,1)}, bf16[4,32,1024]{2,1,0:T(8,128)(2,1)}, u32[]{:S(2)}, u32[]{:S(2)}) collective-permute-start(bf16[4,32,1024]{2,1,0:T(8,128)(2,1)} %collective-permute-done.14.refs_8_), channel_id=1, source_target_pairs={{0,1},{1,0},{2,3},{3,2},{4,5},{5,4},{6,7},{7,6},{8,9},{9,8},{10,11... | collective-permute-start | bytes 786440 | tf_op jit(solution)/shard_map/ppermute | solution.py:44
  63.6 17.3 %collective-permute-start.19 = (bf16[4,32,1024]{2,1,0:T(8,128)(2,1)}, bf16[4,32,1024]{2,1,0:T(8,128)(2,1)}, u32[]{:S(2)}, u32[]{:S(2)}) collective-permute-start(bf16[4,32,1024]{2,1,0:T(8,128)(2,1)} %collective-permute-done.15.refs_9_), channel_id=1, source_target_pairs={{0,1},{1,0},{2,3},{3,2},{4,5},{5,4},{6,7},{7,6},{8,9},{9,8},{10,11... | collective-permute-start | bytes 786440 | tf_op jit(solution)/shard_map/ppermute | solution.py:44
  65.7 15.2 %copy-start.5 = (bf16[4,32,1024]{2,1,0:T(8,128)(2,1)}, bf16[4,32,1024]{2,1,0:T(8,128)(2,1)S(1)}, u32[]{:S(2)}) copy-start(bf16[4,32,1024]{2,1,0:T(8,128)(2,1)S(1)} %get-tuple-element.58.refs_24_) | copy-start | bytes 786436
  65.7 15.2 %copy-start.6 = (bf16[4,32,1024]{2,1,0:T(8,128)(2,1)}, bf16[4,32,1024]{2,1,0:T(8,128)(2,1)S(1)}, u32[]{:S(2)}) copy-start(bf16[4,32,1024]{2,1,0:T(8,128)(2,1)S(1)} %get-tuple-element.59.refs_23_) | copy-start | bytes 786436
  65.7 15.2 %copy-start.7 = (bf16[4,32,1024]{2,1,0:T(8,128)(2,1)}, bf16[4,32,1024]{2,1,0:T(8,128)(2,1)S(1)}, u32[]{:S(2)}) copy-start(bf16[4,32,1024]{2,1,0:T(8,128)(2,1)S(1)} %get-tuple-element.60.refs_22_) | copy-start | bytes 786436
  65.7 27.7 %collective-permute-start.21 = (bf16[4,32,1024]{2,1,0:T(8,128)(2,1)S(1)}, bf16[4,32,1024]{2,1,0:T(8,128)(2,1)}, u32[]{:S(2)}, u32[]{:S(2)}) collective-permute-start(bf16[4,32,1024]{2,1,0:T(8,128)(2,1)S(1)} %get-tuple-element.60.refs_22_), channel_id=1, source_target_pairs={{0,2},{1,3},{2,0},{3,1},{4,6},{5,7},{6,4},{7,5},{8,10},{9,11},{10,... | collective-permute-start | bytes 786440 | tf_op jit(solution)/shard_map/ppermute | solution.py:44
  67.1 1.5 copy-start.20
  67.1 26.3 %collective-permute-start.22 = (bf16[4,32,1024]{2,1,0:T(8,128)(2,1)S(1)}, bf16[4,32,1024]{2,1,0:T(8,128)(2,1)S(1)}, u32[]{:S(2)}, u32[]{:S(2)}) collective-permute-start(bf16[4,32,1024]{2,1,0:T(8,128)(2,1)S(1)} %get-tuple-element.59.refs_23_), channel_id=1, source_target_pairs={{0,4},{1,5},{2,6},{3,7},{4,0},{5,1},{6,2},{7,3},{8,12},{9,13},{10,... | collective-permute-start | bytes 786440 | tf_op jit(solution)/shard_map/ppermute | solution.py:44
  69.3 24.1 %collective-permute-start.23 = (bf16[4,32,1024]{2,1,0:T(8,128)(2,1)S(1)}, bf16[4,32,1024]{2,1,0:T(8,128)(2,1)}, u32[]{:S(2)}, u32[]{:S(2)}) collective-permute-start(bf16[4,32,1024]{2,1,0:T(8,128)(2,1)S(1)} %get-tuple-element.58.refs_24_), channel_id=1, source_target_pairs={{0,6},{1,7},{2,4},{3,5},{4,2},{5,3},{6,0},{7,1},{8,14},{9,15},{10,... | collective-permute-start | bytes 786440 | tf_op jit(solution)/shard_map/ppermute | solution.py:44
  93.2 10.3 %copy-start.15 = (f32[2,1024,32]{1,2,0:T(8,128)S(1)}, f32[2,1024,32]{1,2,0:T(8,128)}, u32[]{:S(2)}) copy-start(f32[2,1024,32]{1,2,0:T(8,128)} %param.25) | copy-start | bytes 786436
  93.2 24.0 %copy-start.1 = (f32[16,32,1024]{2,1,0:T(8,128)S(1)}, f32[16,32,1024]{2,1,0:T(8,128)}, u32[]{:S(2)}) copy-start(f32[16,32,1024]{2,1,0:T(8,128)} %get-tuple-element.40) | copy-start | bytes 6291460
  93.2 24.0 %collective-permute-start.37 = (bf16[16,32,1024]{2,1,0:T(8,128)(2,1)}, bf16[16,32,1024]{2,1,0:T(8,128)(2,1)S(1)}, u32[]{:S(2)}, u32[]{:S(2)}) collective-permute-start(bf16[16,32,1024]{2,1,0:T(8,128)(2,1)} %get-tuple-element.41), channel_id=1, source_target_pairs={{0,1},{1,0},{2,3},{3,2},{4,5},{5,4},{6,7},{7,6},{8,9},{9,8},{10,11... | collective-permute-start | bytes 3145736 | tf_op jit(solution)/shard_map/ppermute | solution.py:44
  94.7 5.6 %collective-permute-start.24 = (bf16[1,32,1024]{2,1,0:T(8,128)(2,1)S(1)}, bf16[1,32,1024]{2,1,0:T(8,128)(2,1)S(1)}, u32[]{:S(2)}, u32[]{:S(2)}) collective-permute-start(bf16[1,32,1024]{2,1,0:T(8,128)(2,1)S(1)} %get-tuple-element.64), channel_id=1, source_target_pairs={{0,8},{1,9},{2,10},{3,11},{4,12},{5,13},{6,14},{7,15},{8,0},{9,1},... | collective-permute-start | bytes 196616 | tf_op jit(solution)/shard_map/ppermute | solution.py:44
  94.8 8.7 %collective-permute-start.25 = (bf16[1,32,1024]{2,1,0:T(8,128)(2,1)S(1)}, bf16[1,32,1024]{2,1,0:T(8,128)(2,1)S(1)}, u32[]{:S(2)}, u32[]{:S(2)}) collective-permute-start(bf16[1,32,1024]{2,1,0:T(8,128)(2,1)S(1)} %get-tuple-element.66), channel_id=1, source_target_pairs={{0,16},{1,17},{2,18},{3,19},{4,20},{5,21},{6,22},{7,23},{8,24},{9,... | collective-permute-start | bytes 196616 | tf_op jit(solution)/shard_map/ppermute | solution.py:44
  96.0 7.5 %collective-permute-start.26 = (bf16[1,32,1024]{2,1,0:T(8,128)(2,1)S(1)}, bf16[1,32,1024]{2,1,0:T(8,128)(2,1)S(1)}, u32[]{:S(2)}, u32[]{:S(2)}) collective-permute-start(bf16[1,32,1024]{2,1,0:T(8,128)(2,1)S(1)} %get-tuple-element.65), channel_id=1, source_target_pairs={{0,24},{1,25},{2,26},{3,27},{4,28},{5,29},{6,30},{7,31},{8,16},{9,... | collective-permute-start | bytes 196616 | tf_op jit(solution)/shard_map/ppermute | solution.py:44
  104.5 4.5 %collective-permute-start.27 = (bf16[1,32,1024]{2,1,0:T(8,128)(2,1)S(1)}, bf16[1,32,1024]{2,1,0:T(8,128)(2,1)S(1)}, u32[]{:S(2)}, u32[]{:S(2)}) collective-permute-start(bf16[1,32,1024]{2,1,0:T(8,128)(2,1)S(1)} %get-tuple-element.49), channel_id=1, source_target_pairs={{0,8},{1,9},{2,10},{3,11},{4,12},{5,13},{6,14},{7,15},{8,0},{9,1},... | collective-permute-start | bytes 196616 | tf_op jit(solution)/shard_map/ppermute | solution.py:44
  106.1 7.5 %collective-permute-start.28 = (bf16[1,32,1024]{2,1,0:T(8,128)(2,1)S(1)}, bf16[1,32,1024]{2,1,0:T(8,128)(2,1)S(1)}, u32[]{:S(2)}, u32[]{:S(2)}) collective-permute-start(bf16[1,32,1024]{2,1,0:T(8,128)(2,1)S(1)} %get-tuple-element.49), channel_id=1, source_target_pairs={{0,16},{1,17},{2,18},{3,19},{4,20},{5,21},{6,22},{7,23},{8,24},{9,... | collective-permute-start | bytes 196616 | tf_op jit(solution)/shard_map/ppermute | solution.py:44
  106.9 6.8 %collective-permute-start.29 = (bf16[1,32,1024]{2,1,0:T(8,128)(2,1)S(1)}, bf16[1,32,1024]{2,1,0:T(8,128)(2,1)S(1)}, u32[]{:S(2)}, u32[]{:S(2)}) collective-permute-start(bf16[1,32,1024]{2,1,0:T(8,128)(2,1)S(1)} %get-tuple-element.49), channel_id=1, source_target_pairs={{0,24},{1,25},{2,26},{3,27},{4,28},{5,29},{6,30},{7,31},{8,16},{9,... | collective-permute-start | bytes 196616 | tf_op jit(solution)/shard_map/ppermute | solution.py:44
  113.7 32.6 %copy-start.3 = (bf16[4,32,1024]{2,1,0:T(8,128)(2,1)}, bf16[4,32,1024]{2,1,0:T(8,128)(2,1)S(1)}, u32[]{:S(2)}) copy-start(bf16[4,32,1024]{2,1,0:T(8,128)(2,1)S(1)} %pad_maximum_fusion.2.refs_3_) | copy-start | bytes 786436
  113.7 9.2 %collective-permute-start.30 = (bf16[4,32,1024]{2,1,0:T(8,128)(2,1)S(1)}, bf16[4,32,1024]{2,1,0:T(8,128)(2,1)S(1)}, u32[]{:S(2)}, u32[]{:S(2)}) collective-permute-start(bf16[4,32,1024]{2,1,0:T(8,128)(2,1)S(1)} %pad_maximum_fusion.2.refs_3_), channel_id=1, source_target_pairs={{0,2},{1,3},{2,0},{3,1},{4,6},{5,7},{6,4},{7,5},{8,10},{9,11},{10,... | collective-permute-start | bytes 786440 | tf_op jit(solution)/shard_map/ppermute | solution.py:44
  115.1 31.2 %collective-permute-start.31 = (bf16[4,32,1024]{2,1,0:T(8,128)(2,1)S(1)}, bf16[4,32,1024]{2,1,0:T(8,128)(2,1)}, u32[]{:S(2)}, u32[]{:S(2)}) collective-permute-start(bf16[4,32,1024]{2,1,0:T(8,128)(2,1)S(1)} %pad_maximum_fusion.2.refs_3_), channel_id=1, source_target_pairs={{0,4},{1,5},{2,6},{3,7},{4,0},{5,1},{6,2},{7,3},{8,12},{9,13},{10,... | collective-permute-start | bytes 786440 | tf_op jit(solution)/shard_map/ppermute | solution.py:44
  115.8 30.6 %collective-permute-start.32 = (bf16[4,32,1024]{2,1,0:T(8,128)(2,1)S(1)}, bf16[4,32,1024]{2,1,0:T(8,128)(2,1)}, u32[]{:S(2)}, u32[]{:S(2)}) collective-permute-start(bf16[4,32,1024]{2,1,0:T(8,128)(2,1)S(1)} %pad_maximum_fusion.2.refs_3_), channel_id=1, source_target_pairs={{0,6},{1,7},{2,4},{3,5},{4,2},{5,3},{6,0},{7,1},{8,14},{9,15},{10,... | collective-permute-start | bytes 786440 | tf_op jit(solution)/shard_map/ppermute | solution.py:44
  117.2 10.2 %copy-start.23 = (f32[2,32]{1,0:T(2,128)S(1)}, f32[2,32]{1,0:T(2,128)}, u32[]{:S(2)}) copy-start(f32[2,32]{1,0:T(2,128)} %param.26) | copy-start | bytes 772
  117.2 12.0 %copy-start.24 = (s32[1,32,2]{1,2,0:T(2,128)S(1)}, s32[1,32,2]{1,2,0:T(2,128)}, u32[]{:S(2)}) copy-start(s32[1,32,2]{1,2,0:T(2,128)} %param.18) | copy-start | bytes 772
  118.5 28.4 %collective-permute-start.38 = (bf16[4,32,1024]{2,1,0:T(8,128)(2,1)}, bf16[4,32,1024]{2,1,0:T(8,128)(2,1)}, u32[]{:S(2)}, u32[]{:S(2)}) collective-permute-start(bf16[4,32,1024]{2,1,0:T(8,128)(2,1)} %get-tuple-element.42), channel_id=1, source_target_pairs={{0,2},{1,3},{2,0},{3,1},{4,6},{5,7},{6,4},{7,5},{8,10},{9,11},{10,... | collective-permute-start | bytes 786440 | tf_op jit(solution)/shard_map/ppermute | solution.py:44
  119.8 27.2 %collective-permute-start.39 = (bf16[4,32,1024]{2,1,0:T(8,128)(2,1)S(1)}, bf16[4,32,1024]{2,1,0:T(8,128)(2,1)}, u32[]{:S(2)}, u32[]{:S(2)}) collective-permute-start(bf16[4,32,1024]{2,1,0:T(8,128)(2,1)S(1)} %get-tuple-element.43), channel_id=1, source_target_pairs={{0,4},{1,5},{2,6},{3,7},{4,0},{5,1},{6,2},{7,3},{8,12},{9,13},{10,... | collective-permute-start | bytes 786440 | tf_op jit(solution)/shard_map/ppermute | solution.py:44
  122.9 24.5 %collective-permute-start.40 = (bf16[4,32,1024]{2,1,0:T(8,128)(2,1)S(1)}, bf16[4,32,1024]{2,1,0:T(8,128)(2,1)}, u32[]{:S(2)}, u32[]{:S(2)}) collective-permute-start(bf16[4,32,1024]{2,1,0:T(8,128)(2,1)S(1)} %get-tuple-element.44), channel_id=1, source_target_pairs={{0,6},{1,7},{2,4},{3,5},{4,2},{5,3},{6,0},{7,1},{8,14},{9,15},{10,... | collective-permute-start | bytes 786440 | tf_op jit(solution)/shard_map/ppermute | solution.py:44
  124.4 14.2 %all-to-all-start.1 = ((f32[32,8,128]{2,1,0:T(8,128)}), f32[32,8,128]{2,1,0:T(8,128)S(1)}, u32[]{:S(2)}, u32[]{:S(2)}) async-start(f32[32,8,128]{2,1,0:T(8,128)} %bitcast.8), calls=%async_computation.1 | async-start | bytes 262144 | tf_op jit(solution)/shard_map/all_to_all | solution.py:95
  141.3 12.6 %copy-start.26 = (f32[1,128]{1,0:T(1,128)S(1)}, f32[1,128]{1,0:T(1,128)}, u32[]{:S(2)}) copy-start(f32[1,128]{1,0:T(1,128)} %get-tuple-element.46) | copy-start | bytes 1540
  141.3 16.1 %all-to-all-start.2 = ((f32[32,8,128]{2,1,0:T(8,128)}), f32[32,8,128]{2,1,0:T(8,128)S(1)}, u32[]{:S(2)}, u32[]{:S(2)}) async-start(f32[32,8,128]{2,1,0:T(8,128)} %bitcast.32), calls=%async_computation.2 | async-start | bytes 262144 | tf_op jit(solution)/shard_map/all_to_all | solution.py:95
  146.3 4.0 %collective-permute-start.33 = (bf16[4,32,1024]{2,1,0:T(8,128)(2,1)S(1)}, bf16[4,32,1024]{2,1,0:T(8,128)(2,1)S(1)}, u32[]{:S(2)}, u32[]{:S(2)}) collective-permute-start(bf16[4,32,1024]{2,1,0:T(8,128)(2,1)S(1)} %pad_maximum_fusion.2.refs_3_), channel_id=1, source_target_pairs={{0,1},{1,0},{2,3},{3,2},{4,5},{5,4},{6,7},{7,6},{8,9},{9,8},{10,11... | collective-permute-start | bytes 786440 | tf_op jit(solution)/shard_map/ppermute | solution.py:44
  146.4 7.1 %collective-permute-start.34 = (bf16[4,32,1024]{2,1,0:T(8,128)(2,1)}, bf16[4,32,1024]{2,1,0:T(8,128)(2,1)}, u32[]{:S(2)}, u32[]{:S(2)}) collective-permute-start(bf16[4,32,1024]{2,1,0:T(8,128)(2,1)} %copy-done.18), channel_id=1, source_target_pairs={{0,1},{1,0},{2,3},{3,2},{4,5},{5,4},{6,7},{7,6},{8,9},{9,8},{10,11... | collective-permute-start | bytes 786440 | tf_op jit(solution)/shard_map/ppermute | solution.py:44
  146.9 10.5 %collective-permute-start.35 = (bf16[4,32,1024]{2,1,0:T(8,128)(2,1)}, bf16[4,32,1024]{2,1,0:T(8,128)(2,1)}, u32[]{:S(2)}, u32[]{:S(2)}) collective-permute-start(bf16[4,32,1024]{2,1,0:T(8,128)(2,1)} %collective-permute-done.31.refs_5_), channel_id=1, source_target_pairs={{0,1},{1,0},{2,3},{3,2},{4,5},{5,4},{6,7},{7,6},{8,9},{9,8},{10,11... | collective-permute-start | bytes 786440 | tf_op jit(solution)/shard_map/ppermute | solution.py:44
  147.0 10.4 %collective-permute-start.36 = (bf16[4,32,1024]{2,1,0:T(8,128)(2,1)}, bf16[4,32,1024]{2,1,0:T(8,128)(2,1)}, u32[]{:S(2)}, u32[]{:S(2)}) collective-permute-start(bf16[4,32,1024]{2,1,0:T(8,128)(2,1)} %collective-permute-done.32.refs_6_), channel_id=1, source_target_pairs={{0,1},{1,0},{2,3},{3,2},{4,5},{5,4},{6,7},{7,6},{8,9},{9,8},{10,11... | collective-permute-start | bytes 786440 | tf_op jit(solution)/shard_map/ppermute | solution.py:44
  148.7 14.1 %collective-permute-start.41 = (bf16[1,32,1024]{2,1,0:T(8,128)(2,1)S(1)}, bf16[1,32,1024]{2,1,0:T(8,128)(2,1)S(1)}, u32[]{:S(2)}, u32[]{:S(2)}) collective-permute-start(bf16[1,32,1024]{2,1,0:T(8,128)(2,1)S(1)} %get-tuple-element.61), channel_id=1, source_target_pairs={{0,8},{1,9},{2,10},{3,11},{4,12},{5,13},{6,14},{7,15},{8,0},{9,1},... | collective-permute-start | bytes 196616 | tf_op jit(solution)/shard_map/ppermute | solution.py:44
  151.1 11.7 %collective-permute-start.42 = (bf16[1,32,1024]{2,1,0:T(8,128)(2,1)S(1)}, bf16[1,32,1024]{2,1,0:T(8,128)(2,1)S(1)}, u32[]{:S(2)}, u32[]{:S(2)}) collective-permute-start(bf16[1,32,1024]{2,1,0:T(8,128)(2,1)S(1)} %get-tuple-element.63), channel_id=1, source_target_pairs={{0,16},{1,17},{2,18},{3,19},{4,20},{5,21},{6,22},{7,23},{8,24},{9,... | collective-permute-start | bytes 196616 | tf_op jit(solution)/shard_map/ppermute | solution.py:44
  153.5 9.3 %collective-permute-start.43 = (bf16[1,32,1024]{2,1,0:T(8,128)(2,1)S(1)}, bf16[1,32,1024]{2,1,0:T(8,128)(2,1)S(1)}, u32[]{:S(2)}, u32[]{:S(2)}) collective-permute-start(bf16[1,32,1024]{2,1,0:T(8,128)(2,1)S(1)} %get-tuple-element.62), channel_id=1, source_target_pairs={{0,24},{1,25},{2,26},{3,27},{4,28},{5,29},{6,30},{7,31},{8,16},{9,... | collective-permute-start | bytes 196616 | tf_op jit(solution)/shard_map/ppermute | solution.py:44
  154.6 8.2 %copy-start.17 = (f32[2,1024,32]{1,2,0:T(8,128)S(1)}, f32[2,1024,32]{1,2,0:T(8,128)}, u32[]{:S(2)}) copy-start(f32[2,1024,32]{1,2,0:T(8,128)} %param.27) | copy-start | bytes 786436
  (9 other events, 7.2 us)
